TPU v7x, 256 devices: a whole 4x4x8 slice. The times are simulated.
256 devices in a mesh: pb: 8 (over z_hi, x), col: 32 (over y, z_lo, core).
Axes of the slice: x: 4, y: 4, z: 8 (z_hi: 2, z_lo: 4; z = z_hi * 4 + z_lo), core: 2. Of those that a mesh axis runs over, the one named last changes fastest.
Arguments:
- queries: bfloat16 [16384, 1024], P(('pb', 'col')), may hold values from -64 to 64
- candidates: bfloat16 [32768, 1024], P(('col', 'pb')), may hold values from -5 to 5
- grades: int32 [16384, 32768], P('pb', 'col'), may hold values from 0 to 4
- query_weights: float32 [16384], P('pb'), may hold values from -0.03125 to 0.03125
Outputs:
- losses: float32 [16384], P('pb')
- query_grad: bfloat16 [16384, 1024], P(('pb', 'col'))
- cand_grad: bfloat16 [32768, 1024], P(('col', 'pb'))
All inputs are finite; a program needn't handle non-finite values.
Results may differ from a plain program's by a relative error of at most 0.0071.
Values may be sent and summed in bfloat16 or wider, within the bound.
A program may use at most 128 MiB of HBM per device.

v0:
```python
import math

import jax
import jax.numpy as jnp
from jax import lax
from jax.sharding import Mesh
from jax.sharding import PartitionSpec as P

GRADES = 5
COL = ("col_0", "col_1", "col_2")
PB_COL = ("pb", "col_0", "col_1", "col_2")
COL_PB = ("col_0", "col_1", "col_2", "pb")


lowest = -1e30


def all_in_one(x, axis):
    leaves = jax.tree.leaves(x)
    turns = sorted(range(len(leaves)), key=lambda k: -leaves[k].size)
    width = (1, *leaves[turns[0]].shape)[-1]
    lines = [
        jnp.pad(leaves[k].reshape(-1), (0, -leaves[k].size % width)).reshape(-1, width)
        for k in turns
    ]
    both, at, found = (lax.all_gather(jnp.concatenate(lines), axis), 0, {})
    for k, line in zip(turns, lines):
        share = both[:, at : at + len(line)].reshape(len(both), -1)
        found[k] = share[:, : leaves[k].size].reshape(-1, *leaves[k].shape)
        at += len(line)
    numbers = iter(range(len(leaves)))
    return jax.tree.map(lambda _: found[next(numbers)], x)


def joined_all(x, axes, combine):
    for axis in axes:
        pieces = all_in_one(x, axis)
        x = jax.tree.map(lambda part: part[0], pieces)
        for k in range(1, lax.axis_size(axis)):
            x = combine(x, jax.tree.map(lambda part: part[k], pieces))
    return x


def partner(x, axis, stride):
    return lax.ppermute(x, axis, [(i, i ^ 1 << stride) for i in range(lax.axis_size(axis))])


def grade_levels(maxima, masses, counts):
    levels = []
    running = maxima[0]
    seen_count = counts[0] * 0.0
    for bucket in range(maxima.shape[0]):
        running = jnp.maximum(running, maxima[bucket])
        seen_count = seen_count + counts[bucket]
        summed = masses[0] * jnp.exp(maxima[0] - running)
        for lesser in range(1, bucket + 1):
            summed = summed + masses[lesser] * jnp.exp(maxima[lesser] - running)
        present = seen_count > 0.0
        levels.append(
            jnp.where(present, running + jnp.log(jnp.where(present, summed, 1.0)), running)
        )
    return levels


def slope_factors(maxima, levels, counts):
    factors = []
    for bucket in range(maxima.shape[0]):
        summed = counts[bucket] * jnp.exp(maxima[bucket] - levels[bucket])
        for higher in range(bucket + 1, maxima.shape[0]):
            summed = summed + counts[higher] * jnp.exp(maxima[bucket] - levels[higher])
        factors.append(summed)
    return factors


def local(queries, candidates, grades, query_weights):
    width = queries.shape[1]
    scaling = 1.0 / math.sqrt(width)
    cand_block = lax.all_gather(candidates, "pb", axis=0, tiled=True)
    query_block = lax.all_gather(queries, COL, axis=0, tiled=True)
    scores = jnp.dot(query_block, cand_block.T, preferred_element_type=jnp.float32) * scaling
    members = [grades == bucket for bucket in range(GRADES)]
    totals_local = jnp.sum(scores, axis=1)
    counts_local = jnp.stack([jnp.sum(member.astype(jnp.float32), axis=1) for member in members])
    maxima_local = jnp.stack(
        [jnp.max(jnp.where(member, scores, lowest), axis=1) for member in members]
    )

    def spread_rows(values):
        picked = jnp.zeros(scores.shape, jnp.float32)
        for bucket in range(GRADES):
            picked = jnp.where(members[bucket], values[bucket][:, None], picked)
        return picked

    def masses_from(expo):
        return jnp.stack(
            [jnp.sum(jnp.where(members[bucket], expo, 0.0), axis=1) for bucket in range(GRADES)]
        )

    def combine(former, latter):
        merged = jnp.maximum(former[0], latter[0])
        rescaled = former[1] * jnp.exp(former[0] - merged) + latter[1] * jnp.exp(latter[0] - merged)
        return (merged, rescaled, former[2] + latter[2], former[3] + latter[3])

    expo = jnp.exp(scores - spread_rows(maxima_local))
    maxima, masses, counts, totals = joined_all(
        (maxima_local, masses_from(expo), counts_local, totals_local), COL, combine
    )
    columns_all = grades.shape[1] * lax.axis_size(COL)
    levels = grade_levels(maxima, masses, counts)
    weighted = counts[0] * levels[0]
    for bucket in range(1, GRADES):
        weighted = weighted + counts[bucket] * levels[bucket]
    losses = (weighted - totals) / columns_all
    factors = jnp.stack(slope_factors(maxima, levels, counts))
    scaled_factors = factors * jnp.exp(maxima_local - maxima)
    slopes = (query_weights[:, None] * (spread_rows(scaled_factors) * expo - 1.0)).astype(
        jnp.bfloat16
    )
    col_count = lax.axis_size(COL)
    position = lax.axis_index(COL)
    owner_rows = slopes.shape[0] // col_count
    cand_count = slopes.shape[1]
    parity = position % 2
    grouped = slopes.reshape(col_count // 2, 2, owner_rows, cand_count)
    kept_rows = lax.dynamic_index_in_dim(grouped, parity, 1, keepdims=False)
    given_rows = lax.dynamic_index_in_dim(grouped, 1 - parity, 1, keepdims=False)
    taken_rows, partner_cands = partner((given_rows, cand_block), COL, 0)
    joined_rows = jnp.concatenate([kept_rows, taken_rows], axis=2).reshape(-1, 2 * cand_count)
    joined_cands = jnp.concatenate([cand_block, partner_cands], axis=0)
    partial_value = jnp.dot(joined_rows, joined_cands, preferred_element_type=jnp.float32) * scaling
    partial_value = partial_value.reshape(col_count // 2, owner_rows, width)
    bit_count = col_count.bit_length() - 1
    for bit in range(1, bit_count):
        halves = partial_value.reshape(partial_value.shape[0] // 2, 2, owner_rows, width)
        mine = position // 2**bit % 2
        staying = lax.dynamic_index_in_dim(halves, mine, 1, keepdims=False)
        leaving = lax.dynamic_index_in_dim(halves, 1 - mine, 1, keepdims=False)
        partial_value = staying + partner(leaving.astype(jnp.bfloat16), COL, bit).astype(
            leaving.dtype
        )
    query_grad = partial_value.reshape(owner_rows, width).astype(jnp.bfloat16)
    cand_grad = lax.psum_scatter(
        lax.dot_general(
            slopes, query_block, (((0,), (0,)), ((), ())), preferred_element_type=jnp.float32
        )
        * scaling,
        "pb",
        scatter_dimension=0,
        tiled=True,
    )
    return (losses, query_grad, cand_grad.astype(jnp.bfloat16))


def solution(mesh):
    split = Mesh(mesh.devices.reshape(mesh.shape["pb"], 4, 4, 2), ("pb", "col_0", "col_1", "col_2"))
    return jax.shard_map(
        local,
        mesh=split,
        in_specs=(P(PB_COL, None), P(COL_PB, None), P("pb", COL), P("pb")),
        out_specs=(P("pb"), P(PB_COL, None), P(COL_PB, None)),
        check_vma=False,
    )
```

profile of v0, /device:TPU:1, one launch (start us, length us, event | category | flops | bytes accessed | tf_op | source)
XLA Modules:
  0.0 382.4 jit_solution(16442305566309222181)
XLA Ops:
  7.2 0.0 all-gather.8.cloned.1.call-start
  7.2 0.7 all-gather.8.cloned.1.call-update
  7.9 0.0 all-gather.6.cloned.1.call-start
  7.9 0.7 all-gather.6.cloned.1.call-update
  8.6 0.0 reduce-scatter.2.cloned.1.call-start
  8.7 78.8 %all-gather.8.cloned.1.call-done = bf16[1024,1024]{1,0:T(8,128)(2,1)} async-done(((bf16[128,1024]{1,0:T(8,128)(2,1)}), bf16[1024,1024]{1,0:T(8,128)(2,1)}) %all-gather.8.cloned.1.call-update) | async-done | bytes 2097168 | tf_op jit(solution)/shard_map/all_gather | solution.py:78
  87.5 63.3 %all-gather.6.cloned.1.call-done = bf16[2048,1024]{1,0:T(8,128)(2,1)} async-done(((bf16[64,1024]{1,0:T(8,128)(2,1)}), bf16[2048,1024]{1,0:T(8,128)(2,1)}) %all-gather.6.cloned.1.call-update) | async-done | bytes 4194320 | tf_op jit(solution)/shard_map/all_gather | solution.py:79
  150.8 19.5 %multiply_reduce_fusion = (f32[2048]{0:T(1024)S(1)}, f32[2048]{0:T(1024)S(1)}, f32[2048]{0:T(1024)S(1)}, f32[2048]{0:T(1024)S(1)}, f32[2048]{0:T(1024)S(1)}, /*i...) fusion(s32[2048,1024]{1,0:T(8,128)} %param.6, ...), kind=kOutput, calls=%fused_computation.17 | convolution fusion | flops 4334798848 | bytes 33611776 | tf_op jit(solution)/shard_map/dot_general | solution.py:80
  170.4 19.6 %select_reduce_fusion = (f32[2048]{0:T(1024)S(1)}, f32[2048]{0:T(1024)S(1)}, f32[2048]{0:T(1024)S(1)}, f32[2048]{0:T(1024)S(1)}, f32[2048]{0:T(1024)S(1)}, /*ind...) fusion(pred[2048,1024]{1,0:T(8,128)(4,1)S(1)} %get-tuple-element.35, ...), kind=kLoop, calls=%fused_computation.6 | loop fusion | flops 52410368 | bytes 27377664 | tf_op jit(solution)/shard_map/reduce_sum | solution.py:96
  190.0 0.2 concatenate.21
  190.2 10.2 %all-gather = f32[64,2048]{1,0:T(8,128)S(1)} all-gather(f32[16,2048]{1,0:T(8,128)S(1)} %concatenate.21), channel_id=2, replica_groups=mesh['pb'=8,'col_0'=4,'col_1'=4,'col_2'=2] {'col_0'}, dimensions={0}, use_global_device_ids=true | all-gather | bytes 655360 | tf_op jit(solution)/shard_map/all_gather | solution.py:26
  200.4 0.1 fusion.30
  200.6 13.1 %all-gather.1 = f32[64,2048]{1,0:T(8,128)S(1)} all-gather(f32[16,2048]{1,0:T(8,128)S(1)} %pad_maximum_fusion), channel_id=3, replica_groups=mesh['pb'=8,'col_0'=4,'col_1'=4,'col_2'=2] {'col_1'}, dimensions={0}, use_global_device_ids=true | all-gather | bytes 655360 | tf_op jit(solution)/shard_map/all_gather | solution.py:26
  213.8 0.1 fusion.20
  214.0 7.1 %all-gather.2 = f32[32,2048]{1,0:T(8,128)S(1)} all-gather(f32[16,2048]{1,0:T(8,128)S(1)} %pad_maximum_fusion.1), channel_id=4, replica_groups=mesh['pb'=8,'col_0'=4,'col_1'=4,'col_2'=2] {'col_2'}, dimensions={0}, use_global_device_ids=true | all-gather | bytes 393216 | tf_op jit(solution)/shard_map/all_gather | solution.py:26
  221.1 0.1 stack.74
  221.2 0.2 bitcast_multiply_fusion
  221.4 0.2 fusion.67
  221.5 0.1 fusion.66
  221.7 0.1 fusion.65
  221.8 0.2 fusion.64
  222.0 0.1 stack.73
  222.1 9.9 %multiply_convert_fusion = bf16[2048,1024]{1,0:T(8,128)(2,1)S(1)} fusion(f32[2048,1024]{1,0:T(8,128)} %get-tuple-element.33, pred[2048,1024]{1,0:T(8,128)(4,1)} %copy-done.1, pred[2048,1024]{1,0:T(8,128)(4,1)} %copy-done.2, pred[2048,1024]{1,0:T(8,128)(4,1)} %copy-done.3, pred[2048,1024]{1,0:T(8,128)(4,1)} %copy-done.4, ...), kind=kLoop, calls=%fused_computation | loop fusion | flops 18874368 | bytes 23117824 | tf_op jit(solution)/shard_map/convert_element_type | solution.py:116
  232.1 2.0 copy-done
  234.0 6.1 %convolution_multiply_fusion = f32[1024,1024]{1,0:T(8,128)} fusion(bf16[2048,1024]{1,0:T(8,128)(2,1)S(1)} %multiply_convert_fusion, bf16[2048,1024]{1,0:T(8,128)(2,1)S(1)} %copy-done.7), kind=kOutput, calls=%fused_computation.30 | convolution fusion | flops 4296015872 | bytes 12582912 | tf_op jit(solution)/shard_map/dot_general | solution.py:143
  240.2 0.5 collective-permute-start.1
  240.6 4.2 %constant_dynamic-slice_fusion = (bf16[16,1,64,1024]{3,2,1,0:T(8,128)(2,1)S(1)}, bf16[16,64,1024]{2,1,0:T(8,128)(2,1)}) fusion(bf16[16,2,64,1024]{3,2,1,0:T(8,128)(2,1)} %bitcast.361, s32[]{:T(128)S(6)} %select_n.256, s32[]{:T(128)S(6)} %select_n.257), kind=kLoop, calls=%fused_computation.202 | loop fusion | bytes 8388616 | tf_op jit(solution)/shard_map/jit(dynamic_index_in_dim)/dynamic_slice | solution.py:125
  244.8 0.1 collective-permute-start
  245.0 4.4 %collective-permute-done = bf16[16,64,1024]{2,1,0:T(8,128)(2,1)} collective-permute-done((bf16[16,64,1024]{2,1,0:T(8,128)(2,1)}, bf16[16,64,1024]{2,1,0:T(8,128)(2,1)}, u32[]{:S(2)}, u32[]{:S(2)}) %collective-permute-start) | collective-permute-done | bytes 2097184 | tf_op jit(solution)/shard_map/ppermute | solution.py:45
  249.3 7.7 %broadcast_multiply_fusion = f32[1024,1024]{1,0:T(8,128)S(1)} fusion(bf16[1024,1024]{1,0:T(8,128)(2,1)} %collective-permute-done.1, bf16[1024,1024]{1,0:T(8,128)(2,1)} %all-gather.8.cloned.1.call-done, bf16[1024,1024]{1,0:T(8,128)(2,1)} %bitcast.72, bf16[1024,1024]{1,0:T(8,128)(2,1)S(1)} %bitcast.374), kind=kOutput, calls=%fused_computation.33 | convolution fusion | flops 4312793088 | bytes 12582912 | tf_op jit(solution)/shard_map/dot_general | solution.py:130
  257.0 2.0 copy-done.5
  259.0 0.1 fusion.11
  259.2 0.1 collective-permute-start.2
  259.3 45.4 %collective-permute-done.2 = bf16[8,64,1024]{2,1,0:T(8,128)(2,1)S(1)} collective-permute-done((bf16[8,64,1024]{2,1,0:T(8,128)(2,1)S(1)}, bf16[8,64,1024]{2,1,0:T(8,128)(2,1)S(1)}, u32[]{:S(2)}, u32[]{:S(2)}) %collective-permute-start.2) | collective-permute-done | bytes 1048608 | tf_op jit(solution)/shard_map/ppermute | solution.py:45
  304.7 1.9 bitcast_add_fusion
  306.5 0.1 fusion.12
  306.6 0.1 collective-permute-start.3
  306.8 39.6 %collective-permute-done.3 = bf16[4,64,1024]{2,1,0:T(8,128)(2,1)S(1)} collective-permute-done((bf16[4,64,1024]{2,1,0:T(8,128)(2,1)S(1)}, bf16[4,64,1024]{2,1,0:T(8,128)(2,1)S(1)}, u32[]{:S(2)}, u32[]{:S(2)}) %collective-permute-start.3) | collective-permute-done | bytes 524320 | tf_op jit(solution)/shard_map/ppermute | solution.py:45
  346.4 0.2 bitcast_add_fusion.1
  346.7 0.1 collective-permute-start.4
  346.8 7.4 %collective-permute-done.4 = bf16[2,64,1024]{2,1,0:T(8,128)(2,1)S(1)} collective-permute-done((bf16[2,64,1024]{2,1,0:T(8,128)(2,1)S(1)}, bf16[2,64,1024]{2,1,0:T(8,128)(2,1)S(1)}, u32[]{:S(2)}, u32[]{:S(2)}) %collective-permute-start.4) | collective-permute-done | bytes 262176 | tf_op jit(solution)/shard_map/ppermute | solution.py:45
  354.2 0.1 bitcast_add_fusion.2
  354.3 0.5 collective-permute-start.5
  354.8 0.6 fusion.52
  355.5 4.7 %collective-permute-done.5 = bf16[1,64,1024]{2,1,0:T(8,128)(2,1)S(1)} collective-permute-done((bf16[1,64,1024]{2,1,0:T(8,128)(2,1)S(1)}, bf16[1,64,1024]{2,1,0:T(8,128)(2,1)S(1)}, u32[]{:S(2)}, u32[]{:S(2)}) %collective-permute-start.5) | collective-permute-done | bytes 131104 | tf_op jit(solution)/shard_map/ppermute | solution.py:45
  360.1 0.7 fusion.14
  360.8 13.3 %reduce-scatter.2.cloned.1.call-done = f32[128,1024]{1,0:T(8,128)} async-done(((f32[1024,1024]{1,0:T(8,128)}), f32[128,1024]{1,0:T(8,128)}) %reduce-scatter.2.cloned.1.call-update) | async-done | bytes 524304 | tf_op jit(solution)/shard_map/reduce_scatter | solution.py:142
  374.1 1.8 convert_element_type.81
  (30 shorter events, 0.5 us)
Async XLA Ops:
  7.2 80.4 %all-gather.8.cloned.1.call-start = ((), (), s32[]{:S(2)}) async-start(), calls=%async_computation.2 | async-start | bytes 2359296 | tf_op jit(solution)/shard_map/all_gather | solution.py:78
  7.9 142.9 %all-gather.6.cloned.1.call-start = ((), (), s32[]{:S(2)}) async-start(), calls=%async_computation.1 | async-start | bytes 4325376 | tf_op jit(solution)/shard_map/all_gather | solution.py:79
  8.6 365.4 %reduce-scatter.2.cloned.1.call-start = ((), (), s32[]{:S(2)}) async-start(), calls=%async_computation.3 | async-start | bytes 4718592 | tf_op jit(solution)/shard_map/reduce_scatter | solution.py:142
  170.4 19.6 %copy-start.1 = (pred[2048,1024]{1,0:T(8,128)(4,1)}, pred[2048,1024]{1,0:T(8,128)(4,1)S(1)}, u32[]{:S(2)}) copy-start(pred[2048,1024]{1,0:T(8,128)(4,1)S(1)} %get-tuple-element.35) | copy-start | bytes 6291460
  170.4 19.6 %copy-start.2 = (pred[2048,1024]{1,0:T(8,128)(4,1)}, pred[2048,1024]{1,0:T(8,128)(4,1)S(1)}, u32[]{:S(2)}) copy-start(pred[2048,1024]{1,0:T(8,128)(4,1)S(1)} %get-tuple-element.36) | copy-start | bytes 6291460
  170.4 19.6 %copy-start.3 = (pred[2048,1024]{1,0:T(8,128)(4,1)}, pred[2048,1024]{1,0:T(8,128)(4,1)S(1)}, u32[]{:S(2)}) copy-start(pred[2048,1024]{1,0:T(8,128)(4,1)S(1)} %get-tuple-element.37) | copy-start | bytes 6291460
  170.4 19.6 %copy-start.4 = (pred[2048,1024]{1,0:T(8,128)(4,1)}, pred[2048,1024]{1,0:T(8,128)(4,1)S(1)}, u32[]{:S(2)}) copy-start(pred[2048,1024]{1,0:T(8,128)(4,1)S(1)} %get-tuple-element.38) | copy-start | bytes 6291460
  190.0 32.1 %copy-start.6 = (f32[2048]{0:T(1024)S(1)}, f32[2048]{0:T(1024)}, u32[]{:S(2)}) copy-start(f32[2048]{0:T(1024)} %param.7) | copy-start | bytes 24580
  222.1 11.9 %copy-start.7 = (bf16[2048,1024]{1,0:T(8,128)(2,1)S(1)}, bf16[2048,1024]{1,0:T(8,128)(2,1)}, u32[]{:S(2)}) copy-start(bf16[2048,1024]{1,0:T(8,128)(2,1)} %all-gather.6.cloned.1.call-done) | copy-start | bytes 12582916
  232.0 2.0 copy-start
  240.2 4.8 %collective-permute-start.1 = (bf16[1024,1024]{1,0:T(8,128)(2,1)}, bf16[1024,1024]{1,0:T(8,128)(2,1)}, u32[]{:S(2)}, u32[]{:S(2)}) collective-permute-start(bf16[1024,1024]{1,0:T(8,128)(2,1)} %all-gather.8.cloned.1.call-done), channel_id=1, source_target_pairs={{0,1},{1,0},{2,3},{3,2},{4,5},{5,4},{6,7},{7,6},{8,9},{9,8},{10,11... | collective-permute-start | bytes 6291464 | tf_op jit(solution)/shard_map/ppermute | solution.py:45
  244.8 4.5 %collective-permute-start = (bf16[16,64,1024]{2,1,0:T(8,128)(2,1)}, bf16[16,64,1024]{2,1,0:T(8,128)(2,1)}, u32[]{:S(2)}, u32[]{:S(2)}) collective-permute-start(bf16[16,64,1024]{2,1,0:T(8,128)(2,1)} %get-tuple-element.40), channel_id=1, source_target_pairs={{0,1},{1,0},{2,3},{3,2},{4,5},{5,4},{6,7},{7,6},{8,9},{9,8},{10,11... | collective-permute-start | bytes 6291464 | tf_op jit(solution)/shard_map/ppermute | solution.py:45
  257.0 2.0 copy-start.5
  259.2 45.5 %collective-permute-start.2 = (bf16[8,64,1024]{2,1,0:T(8,128)(2,1)S(1)}, bf16[8,64,1024]{2,1,0:T(8,128)(2,1)S(1)}, u32[]{:S(2)}, u32[]{:S(2)}) collective-permute-start(bf16[8,64,1024]{2,1,0:T(8,128)(2,1)S(1)} %fusion.11), channel_id=1, source_target_pairs={{0,2},{1,3},{2,0},{3,1},{4,6},{5,7},{6,4},{7,5},{8,10},{9,11},{10,... | collective-permute-start | bytes 3145736 | tf_op jit(solution)/shard_map/ppermute | solution.py:45
  306.6 39.8 %collective-permute-start.3 = (bf16[4,64,1024]{2,1,0:T(8,128)(2,1)S(1)}, bf16[4,64,1024]{2,1,0:T(8,128)(2,1)S(1)}, u32[]{:S(2)}, u32[]{:S(2)}) collective-permute-start(bf16[4,64,1024]{2,1,0:T(8,128)(2,1)S(1)} %fusion.12), channel_id=1, source_target_pairs={{0,4},{1,5},{2,6},{3,7},{4,0},{5,1},{6,2},{7,3},{8,12},{9,13},{10,... | collective-permute-start | bytes 1572872 | tf_op jit(solution)/shard_map/ppermute | solution.py:45
  346.7 7.6 %collective-permute-start.4 = (bf16[2,64,1024]{2,1,0:T(8,128)(2,1)S(1)}, bf16[2,64,1024]{2,1,0:T(8,128)(2,1)S(1)}, u32[]{:S(2)}, u32[]{:S(2)}) collective-permute-start(bf16[2,64,1024]{2,1,0:T(8,128)(2,1)S(1)} %fusion.13), channel_id=1, source_target_pairs={{0,8},{1,9},{2,10},{3,11},{4,12},{5,13},{6,14},{7,15},{8,0},{9,1},... | collective-permute-start | bytes 786440 | tf_op jit(solution)/shard_map/ppermute | solution.py:45
  354.3 5.8 %collective-permute-start.5 = (bf16[1,64,1024]{2,1,0:T(8,128)(2,1)S(1)}, bf16[1,64,1024]{2,1,0:T(8,128)(2,1)S(1)}, u32[]{:S(2)}, u32[]{:S(2)}) collective-permute-start(bf16[1,64,1024]{2,1,0:T(8,128)(2,1)S(1)} %dynamic-slice_convert_fusion.2), channel_id=1, source_target_pairs={{0,16},{1,17},{2,18},{3,19},{4,20},{5,21},{6,22},{7,23},{8,24},{9,... | collective-permute-start | bytes 393224 | tf_op jit(solution)/shard_map/ppermute | solution.py:45
Sparse Core Ops, SparseCore 0:
  10.6 76.8 all-gather.7
  89.4 61.3 all-gather.5
  240.3 133.7 reduce-scatter.1
where the time goes:
time: 383 us; the launch traced here: 382 us
  waiting for transfers between devices  258 us (67%)
  other arithmetic  35.9 us (9%)
  matrix products  33.4 us (9%)
  blocking collectives  30.4 us (8%)
  between operations  14.2 us (4%)
  local copies, waits for them, and re-layouts  8.83 us (2%)
    ppermute x6, waiting for transfers between devices, partner(): lax.ppermute(x, axis, [(i, i ^ 1 << stride) for i in range(lax.axis_size(...  101 us
    all_gather x1, waiting for transfers between devices, local(): cand_block = lax.all_gather(candidates, 'pb', axis=0, tiled=True)  78.8 us
    all_gather x1, waiting for transfers between devices, local(): query_block = lax.all_gather(queries, COL, axis=0, tiled=True)  63.3 us
    all_gather x3, blocking collectives, all_in_one(): both, at, found = (lax.all_gather(jnp.concatenate(lines), axis), 0, {})  30.4 us
    reduce_sum x1, other arithmetic, masses_from(): jnp.sum(jnp.where(members[bucket], expo, 0.0), axis=1)  19.6 us
    dot_general x1, matrix products, local(): jnp.dot(query_block, cand_block.T, preferred_element_type=jnp.float32)  19.5 us
    reduce_scatter x1, waiting for transfers between devices, local(): lax.psum_scatter(lax.dot_general(slopes, query_block, (((0,), (0,)), ((),...  13.3 us
    convert_element_type x1, other arithmetic, local(): (query_weights[:, None] * (spread_rows(scaled_factors) * expo - 1.0)).ast...  9.92 us
  transfers between devices with their start and end apart: 9, of which 8 were waited for; matrix products, arithmetic and copies ran while one was open for 4% of the time, Pallas kernels for 0%

commit v1 on v0

v1 whole, which is shorter than its diff:
```python
import jax
import jax.numpy as jnp
from jax import lax
from jax.experimental import pallas as pl
from jax.experimental.pallas import tpu as pltpu
from jax.sharding import Mesh
from jax.sharding import PartitionSpec as P

GRADES = 5
LOWEST = -1e30
AXES = ("zh", "x", "y", "zl", "c")
ROWS = ("zh", "x")
COL = ("y", "zl", "c")
SCALE = 1.0 / 32.0
EXP2_SCALE = 1.4426950408889634 / 32.0
BF = jnp.bfloat16
F32 = jnp.float32
LANES = 128


class Wires:
    def __init__(self, send_sems, recv_sems):
        self.send_sems, self.recv_sems = send_sems, recv_sems
        self.names, self.sent = {}, []

    def slot(self, name):
        return self.names.setdefault(name, len(self.names))

    def send(self, src, dst, name, where):
        copy = pltpu.make_async_remote_copy(
            src_ref=src,
            dst_ref=dst,
            send_sem=self.send_sems.at[len(self.sent)],
            recv_sem=self.recv_sems.at[self.slot(name)],
            device_id=where,
            device_id_type=pl.DeviceIdType.MESH,
        )
        copy.start()
        self.sent.append(copy)

    def arrive(self, dst, name, where):
        pltpu.make_async_remote_copy(
            src_ref=dst,
            dst_ref=dst,
            send_sem=self.send_sems.at[0],
            recv_sem=self.recv_sems.at[self.slot(name)],
            device_id=where,
            device_id_type=pl.DeviceIdType.MESH,
        ).wait_recv()

    def finish(self):
        for copy in self.sent:
            copy.wait_send()


def combine(parts):
    row = lax.broadcasted_iota(jnp.int32, (8, LANES), 0)
    stat = row < GRADES
    top = parts[0][0]
    for first, _ in parts[1:]:
        top = jnp.maximum(top, first)
    plain = jnp.zeros((8, LANES), F32)
    mass = jnp.zeros((8, LANES), F32)
    for first, second in parts:
        plain = plain + first
        mass = mass + second * jnp.where(stat, jnp.exp(first - top), 1.0)
    return jnp.where(stat, top, plain), mass


def stacked(rows):
    row = lax.broadcasted_iota(jnp.int32, (8, LANES), 0)
    out = jnp.zeros((8, LANES), F32)
    for k, value in enumerate(rows):
        out = jnp.where(row == k, value, out)
    return out


def outcome(first, second, columns):
    maxima = [first[k : k + 1] for k in range(GRADES)]
    masses = [second[k : k + 1] for k in range(GRADES)]
    counts = [first[5:6], first[6:7], first[7:8], second[5:6], second[6:7]]
    totals = second[7:8]
    levels, running, seen = [], maxima[0], jnp.zeros_like(totals)
    for k in range(GRADES):
        running = jnp.maximum(running, maxima[k])
        seen = seen + counts[k]
        summed = masses[0] * jnp.exp(maxima[0] - running)
        for h in range(1, k + 1):
            summed = summed + masses[h] * jnp.exp(maxima[h] - running)
        present = seen > 0.0
        levels.append(jnp.where(present, running + jnp.log(jnp.where(present, summed, 1.0)), running))
    weighted = counts[0] * levels[0]
    for k in range(1, GRADES):
        weighted = weighted + counts[k] * levels[k]
    losses = (weighted - totals) / columns
    factors = []
    for h in range(GRADES):
        summed = counts[h] * jnp.exp(maxima[h] - levels[h])
        for k in range(h + 1, GRADES):
            summed = summed + counts[k] * jnp.exp(maxima[h] - levels[k])
        factors.append(summed)
    return stacked(maxima), stacked(factors + [losses])


def spread(table, grade):
    return jnp.take_along_axis(table, grade, axis=0, mode="promise_in_bounds")


def kernel(
    q_ref, c_ref, w_ref, g_hbm, loss_ref, qg_ref, cg_ref,
    q_all, c_all, c_par, g_in, g_t, es, sl, sl_par, z_rel, tab, cnt, st, st_in, st_core, res,
    q_part, q_s1, q_r1, q_s2, q_r2, q_s3, q_r3,
    c_part, c_s1, c_r1, c_s2, c_r2, c_s3, c_rel, c_r3,
    send_sems, recv_sems, g_sems,
):
    zh, x, y, zl, c = (lax.axis_index(a) for a in AXES)
    other = 1 - c
    wires = Wires(send_sems, recv_sems)
    send, arrive = wires.send, wires.arrive
    up_y, dn_y = {"y": (y + 1) % 4}, {"y": (y + 3) % 4}
    up_x, dn_x = {"x": (x + 1) % 4}, {"x": (x + 3) % 4}
    mate = {"c": other}
    zl2 = (zl + 2) % 4
    up_zh, dn_zh = (zh + zl // 2) % 2, (zh + 1 + zl // 2) % 2
    up_z, dn_z = {"zh": up_zh, "zl": zl2}, {"zh": dn_zh, "zl": zl2}

    def peer(dy, dz):
        return {"y": (y + dy) % 4, "zl": (zl + dz) % 4}

    others = [(dy, dz) for dy in range(4) for dz in range(4) if (dy, dz) != (0, 0)]

    def q_rows(core, k, dy, start=0, size=64):
        at = core * 1024 + (zl + k) % 4 * 256 + (y + dy) % 4 * 64 + start
        return q_all.at[pl.ds(pl.multiple_of(at, 32), size), :]

    def c_rows(half, dx, start=0, size=128):
        at = half * 512 + (x + dx) % 4 * 128 + start
        return c_all.at[pl.ds(pl.multiple_of(at, 64), size), :]

    def grade_copies(tile):
        core, plane, pair = tile // 8, tile // 2 % 4, tile % 2
        copies = []
        for i in range(2):
            at = (((pair * 2 + i) * 4 + plane) * 2 + core) * 64
            copies.append(
                pltpu.make_async_copy(
                    g_hbm.at[pl.ds(at, 64), :],
                    g_in.at[tile % 4, pl.ds(64 * i, 64), :],
                    g_sems.at[tile % 4, i],
                )
            )
        return copies

    for tile in range(4):
        for copy in grade_copies(tile):
            copy.start()

    barrier = pltpu.get_barrier_semaphore()
    greeted = [peer(dy, dz) for dy, dz in others] + [up_x, dn_x, mate, {"zh": 1 - zh, "zl": zl2}]
    for device in greeted:
        pl.semaphore_signal(barrier, inc=1, device_id=device, device_id_type=pl.DeviceIdType.MESH)
    pl.semaphore_wait(barrier, len(greeted))

    send(q_ref, q_rows(c, 0, 0), ("qy", 0, 0), up_y)
    send(q_ref, q_rows(c, 0, 0), ("qy", 0, 1), dn_y)
    send(c_ref, c_rows(zh, 0), ("cx", 0), up_x)
    send(c_ref, c_rows(zh, 0), ("cx", 1), dn_x)
    send(c_ref.at[pl.ds(0, 64), :], z_rel.at[0], ("zr", 0), up_z)
    send(c_ref.at[pl.ds(64, 64), :], z_rel.at[1], ("zr", 1), dn_z)
    for m in (1, 3, 2):
        send(q_ref, q_rows(c, 0, 0), ("qz", 4 - m), peer(0, m))
    send(q_ref, q_rows(c, 0, 0), ("qd", 0, 0), mate)
    q_rows(c, 0, 0)[...] = q_ref[...]
    c_rows(zh, 0)[...] = c_ref[...]

    def to_mate(k, dy):
        send(q_rows(c, k, dy), q_rows(c, k, dy), ("qd", k, dy), mate)

    def q_near(k):
        arrive(q_rows(c, k, 3), ("qy", k, 0), dn_y)
        send(q_rows(c, k, 3, 0, 32), q_rows(c, k, 3, 0, 32), ("qf", k, 0), up_y)
        to_mate(k, 3)
        arrive(q_rows(c, k, 1), ("qy", k, 1), up_y)
        send(q_rows(c, k, 1, 32, 32), q_rows(c, k, 1, 32, 32), ("qf", k, 1), dn_y)
        to_mate(k, 1)

    def q_far(k):
        arrive(q_rows(c, k, 2, 0, 32), ("qf", k, 0), dn_y)
        arrive(q_rows(c, k, 2, 32, 32), ("qf", k, 1), up_y)
        to_mate(k, 2)

    def q_over(k):
        arrive(q_rows(c, k, 0), ("qz", k), peer(0, k))
        send(q_rows(c, k, 0), q_rows(c, k, 0), ("qy", k, 0), up_y)
        send(q_rows(c, k, 0), q_rows(c, k, 0), ("qy", k, 1), dn_y)
        to_mate(k, 0)

    def c_near():
        arrive(c_rows(zh, 3), ("cx", 0), dn_x)
        send(c_rows(zh, 3, 0, 64), c_rows(zh, 3, 0, 64), ("cf", 0), up_x)
        arrive(c_rows(zh, 1), ("cx", 1), up_x)
        send(c_rows(zh, 1, 64, 64), c_rows(zh, 1, 64, 64), ("cf", 1), dn_x)

    def c_far():
        arrive(c_rows(zh, 2, 0, 64), ("cf", 0), dn_x)
        arrive(c_rows(zh, 2, 64, 64), ("cf", 1), up_x)

    def c_relay():
        arrive(z_rel.at[0], ("zr", 0), dn_z)
        send(z_rel.at[0], c_rows(1 - up_zh, 0, 0, 64), ("cz", 0), up_z)
        arrive(z_rel.at[1], ("zr", 1), up_z)
        send(z_rel.at[1], c_rows(1 - dn_zh, 0, 64, 64), ("cz", 1), dn_z)

    def c_over():
        for h, frm in ((0, dn_z), (1, up_z)):
            part = c_rows(1 - zh, 0, 64 * h, 64)
            arrive(part, ("cz", h), frm)
            send(part, part, ("px", h, 0), up_x)
            send(part, part, ("px", h, 1), dn_x)

    def p_near():
        for h in range(2):
            arrive(c_rows(1 - zh, 3, 64 * h, 64), ("px", h, 0), dn_x)
            if h == 0:
                part = c_rows(1 - zh, 3, 0, 64)
                send(part, part, ("pf", 0), up_x)
            arrive(c_rows(1 - zh, 1, 64 * h, 64), ("px", h, 1), up_x)
            if h == 1:
                part = c_rows(1 - zh, 1, 64, 64)
                send(part, part, ("pf", 1), dn_x)

    def p_far():
        arrive(c_rows(1 - zh, 2, 0, 64), ("pf", 0), dn_x)
        arrive(c_rows(1 - zh, 2, 64, 64), ("pf", 1), up_x)

    def turn(tile):
        for copy in grade_copies(tile):
            copy.wait()
        for b in range(8):
            block = g_in[tile % 4, :, pl.ds(128 * b, 128)]
            g_t[pl.ds(128 * b, 128), pl.ds(128 * tile, 128)] = jnp.transpose(block)
        if tile + 4 < 16:
            for copy in grade_copies(tile + 4):
                copy.start()

        def tally(i, held):
            held = list(held)
            for j in range(8):
                at = pl.multiple_of(i * 64 + 8 * j, 8)
                grade = g_t[pl.ds(at, 8), pl.ds(128 * tile, 128)]
                for k in range(4):
                    held[k] = held[k] + jnp.where(grade == k, 1.0, 0.0)
            return tuple(held)

        held = lax.fori_loop(0, 16, tally, (jnp.zeros((8, LANES), F32),) * 4)
        held = [jnp.sum(v, axis=0, keepdims=True) for v in held]
        held.append(1024.0 - (held[0] + held[1] + held[2] + held[3]))
        cnt[tile] = stacked(held)

    steps = [
        lambda: q_near(0), c_near, c_relay, lambda: q_over(1), lambda: q_over(3), lambda: q_far(0), c_far,
        lambda: q_over(2), lambda: q_near(1), lambda: q_near(3), c_over, lambda: q_near(2), p_near,
        lambda: q_far(1), lambda: q_far(3), lambda: q_far(2), p_far,
    ]
    for n, step in enumerate(steps):
        if n < 16:
            turn(n)
        step()
    send(c_all, c_par, ("cp",), mate)
    for k in range(4):
        for dy in range(4):
            arrive(q_rows(other, k, dy), ("qd", k, dy), mate)

    tab[...] = jnp.zeros_like(tab)

    def tile_stats(tile):
        lanes = pl.ds(pl.multiple_of(tile * LANES, LANES), LANES)

        def highest(i, held):
            held = list(held)
            for j in range(8):
                at = pl.ds(pl.multiple_of(i * 64 + 8 * j, 8), 8)
                score, grade = es[at, lanes], g_t[at, lanes]
                for k in range(GRADES):
                    held[k] = jnp.maximum(held[k], jnp.where(grade == k, score, 32.0 * LOWEST))
                held[GRADES] = held[GRADES] + score
            return tuple(held)

        low = jnp.full((8, LANES), 32.0 * LOWEST, F32)
        held = lax.fori_loop(0, 16, highest, (low,) * GRADES + (jnp.zeros((8, LANES), F32),))
        maxima = [jnp.max(v, axis=0, keepdims=True) for v in held[:GRADES]]
        total = jnp.sum(held[GRADES], axis=0, keepdims=True) * SCALE
        table = stacked(maxima)

        def masses_of(i, held):
            held = list(held)
            for j in range(8):
                at = pl.ds(pl.multiple_of(i * 64 + 8 * j, 8), 8)
                score, grade = es[at, lanes], g_t[at, lanes]
                value = jnp.exp2((score - spread(table, grade)) * EXP2_SCALE)
                es[at, lanes] = value
                for k in range(GRADES):
                    held[k] = held[k] + jnp.where(grade == k, value, 0.0)
            return tuple(held)

        held = lax.fori_loop(0, 16, masses_of, (jnp.zeros((8, LANES), F32),) * GRADES)
        masses = [jnp.sum(v, axis=0, keepdims=True) for v in held]
        counts = [cnt[tile, pl.ds(k, 1), :] for k in range(GRADES)]
        st[tile, pl.ds(0, 8), :] = stacked([m * SCALE for m in maxima] + counts[:3])
        st[tile, pl.ds(8, 8), :] = stacked(masses + counts[3:] + [total])

    def score_tile(n, _):
        rows = pl.ds(pl.multiple_of(n * 256, 256), 256)
        es[:, rows] = lax.dot_general(
            c_all[...], q_all[rows, :], (((1,), (1,)), ((), ())), preferred_element_type=F32
        )
        tile_stats(2 * n)
        tile_stats(2 * n + 1)
        return 0

    lax.fori_loop(0, 8, score_tile, 0)

    mine = y * 4 + zl
    for dy, dz in others:
        target = (y + dy) % 4 * 4 + (zl + dz) % 4
        send(st.at[target], st_in.at[dy * 4 + dz], ("st", dy, dz), peer(dy, dz))
    parts = [(st[mine, pl.ds(0, 8), :], st[mine, pl.ds(8, 8), :])]
    for dy, dz in others:
        arrive(st_in.at[dy * 4 + dz], ("st", dy, dz), peer(4 - dy, 4 - dz))
        parts.append((st_in[dy * 4 + dz, pl.ds(0, 8), :], st_in[dy * 4 + dz, pl.ds(8, 8), :]))
    first, second = combine(parts)
    st_core[0, pl.ds(0, 8), :] = first
    st_core[0, pl.ds(8, 8), :] = second
    send(st_core.at[0], st_core.at[1], ("sd",), mate)
    arrive(st_core.at[1], ("sd",), mate)
    first, second = combine([(first, second), (st_core[1, pl.ds(0, 8), :], st_core[1, pl.ds(8, 8), :])])
    first, second = outcome(first, second, 32768.0)
    res[mine, pl.ds(0, 8), :] = first
    res[mine, pl.ds(8, 8), :] = second
    for dy, dz in others:
        send(res.at[mine], res.at[mine], ("sr", dy, dz), peer(dy, dz))
    arrive(c_par, ("cp",), mate)
    for dy, dz in others:
        source = (y + 4 - dy) % 4 * 4 + (zl + 4 - dz) % 4
        arrive(res.at[source], ("sr", dy, dz), peer(4 - dy, 4 - dz))
    loss_ref[...] = res[:, 13, :]

    def slope_tile(tile):
        lanes = pl.ds(pl.multiple_of(tile * LANES, LANES), LANES)
        weight = w_ref[pl.ds(tile, 1), :] * SCALE
        table = res[tile, pl.ds(8, 8), :] * jnp.exp(st[tile, pl.ds(0, 8), :] - res[tile, pl.ds(0, 8), :])
        row = lax.broadcasted_iota(jnp.int32, (8, LANES), 0)
        table = jnp.where(row < GRADES, table, 0.0) * weight

        def at_rows(i, _):
            for j in range(4):
                at = pl.multiple_of(i * 64 + 16 * j, 16)
                halves = []
                for h in range(2):
                    rows = pl.ds(pl.multiple_of(at + 8 * h, 8), 8)
                    halves.append(spread(table, g_t[rows, lanes]) * es[rows, lanes] - weight)
                sl[pl.ds(at, 16), lanes] = jnp.concatenate(halves, axis=0).astype(BF)
            return 0

        lax.fori_loop(0, 16, at_rows, 0)

    def lanes_of(core, plane):
        return pl.ds(pl.multiple_of(core * 1024 + plane * 256, 256), 256)

    for k in (1, 2, 3, 0):
        plane = (zl + k) % 4
        slope_tile(other * 8 + plane * 2)
        slope_tile(other * 8 + plane * 2 + 1)
        lanes = lanes_of(other, plane)
        send(sl.at[:, lanes], sl_par.at[:, lanes_of(0, plane)], ("sl", k), mate)
    for k in (1, 2, 3, 0):
        plane = (zl + k) % 4
        slope_tile(c * 8 + plane * 2)
        slope_tile(c * 8 + plane * 2 + 1)

    def c_dot(j):
        half = (zh + 1 - j) % 2
        for i in range(2):
            rows = pl.ds(pl.multiple_of(half * 512 + 256 * i, 256), 256)
            c_part[j, pl.ds(256 * i, 256), :] = jnp.dot(sl[rows, :], q_all[...], preferred_element_type=F32)

        def at(d, start, size):
            return pl.ds(pl.multiple_of((x + d) % 4 * 128 + start, 64), size)

        c_s1[j, 0] = c_part[j, at(2, 0, 64), :].astype(BF)
        c_s1[j, 1] = c_part[j, at(2, 64, 64), :].astype(BF)
        send(c_s1.at[j, 0], c_r1.at[j, 0], ("s1", j, 0), up_x)
        send(c_s1.at[j, 1], c_r1.at[j, 1], ("s1", j, 1), dn_x)

    def c_mid(j):
        def at(d, start, size):
            return pl.ds(pl.multiple_of((x + d) % 4 * 128 + start, 64), size)

        arrive(c_r1.at[j, 0], ("s1", j, 0), dn_x)
        c_s2[j, 0, pl.ds(0, 64), :] = (c_part[j, at(1, 0, 64), :] + c_r1[j, 0].astype(F32)).astype(BF)
        c_s2[j, 0, pl.ds(64, 64), :] = c_part[j, at(1, 64, 64), :].astype(BF)
        send(c_s2.at[j, 0], c_r2.at[j, 0], ("s2", j, 0), up_x)
        arrive(c_r1.at[j, 1], ("s1", j, 1), up_x)
        c_s2[j, 1, pl.ds(0, 64), :] = c_part[j, at(3, 0, 64), :].astype(BF)
        c_s2[j, 1, pl.ds(64, 64), :] = (c_part[j, at(3, 64, 64), :] + c_r1[j, 1].astype(F32)).astype(BF)
        send(c_s2.at[j, 1], c_r2.at[j, 1], ("s2", j, 1), dn_x)

    def c_sum(j):
        arrive(c_r2.at[j, 0], ("s2", j, 0), dn_x)
        arrive(c_r2.at[j, 1], ("s2", j, 1), up_x)
        at = pl.ds(pl.multiple_of(x * 128, 128), 128)
        return c_part[j, at, :] + c_r2[j, 0].astype(F32) + c_r2[j, 1].astype(F32)

    def c_leave():
        c_s3[...] = c_sum(0).astype(BF)
        send(c_s3.at[pl.ds(0, 64), :], c_rel.at[0], ("t1", 0), up_z)
        send(c_s3.at[pl.ds(64, 64), :], c_rel.at[1], ("t1", 1), dn_z)

    def c_pass():
        arrive(c_rel.at[0], ("t1", 0), dn_z)
        send(c_rel.at[0], c_r3.at[pl.ds(0, 64), :], ("t2", 0), up_z)
        arrive(c_rel.at[1], ("t1", 1), up_z)
        send(c_rel.at[1], c_r3.at[pl.ds(64, 64), :], ("t2", 1), dn_z)

    def c_end():
        total = c_sum(1)
        arrive(c_r3.at[pl.ds(0, 64), :], ("t2", 0), dn_z)
        arrive(c_r3.at[pl.ds(64, 64), :], ("t2", 1), up_z)
        cg_ref[...] = (total + c_r3[...].astype(F32)).astype(BF)

    dims = (((0,), (0,)), ((), ()))

    def q_dot(k):
        plane = (zl + k) % 4
        arrive(sl_par.at[:, lanes_of(0, plane)], ("sl", k), mate)
        q_part[k] = lax.dot_general(
            sl[:, lanes_of(c, plane)], c_all[...], dims, preferred_element_type=F32
        ) + lax.dot_general(sl_par[:, lanes_of(0, plane)], c_par[...], dims, preferred_element_type=F32)

        def at(d, start, size):
            return pl.ds(pl.multiple_of((y + d) % 4 * 64 + start, 32), size)

        q_s1[k, 0] = q_part[k, at(2, 0, 32), :].astype(BF)
        q_s1[k, 1] = q_part[k, at(2, 32, 32), :].astype(BF)
        send(q_s1.at[k, 0], q_r1.at[k, 0], ("r1", k, 0), up_y)
        send(q_s1.at[k, 1], q_r1.at[k, 1], ("r1", k, 1), dn_y)

    def q_mid(k):
        def at(d, start, size):
            return pl.ds(pl.multiple_of((y + d) % 4 * 64 + start, 32), size)

        arrive(q_r1.at[k, 0], ("r1", k, 0), dn_y)
        q_s2[k, 0, pl.ds(0, 32), :] = (q_part[k, at(1, 0, 32), :] + q_r1[k, 0].astype(F32)).astype(BF)
        q_s2[k, 0, pl.ds(32, 32), :] = q_part[k, at(1, 32, 32), :].astype(BF)
        send(q_s2.at[k, 0], q_r2.at[k, 0], ("r2", k, 0), up_y)
        arrive(q_r1.at[k, 1], ("r1", k, 1), up_y)
        q_s2[k, 1, pl.ds(0, 32), :] = q_part[k, at(3, 0, 32), :].astype(BF)
        q_s2[k, 1, pl.ds(32, 32), :] = (q_part[k, at(3, 32, 32), :] + q_r1[k, 1].astype(F32)).astype(BF)
        send(q_s2.at[k, 1], q_r2.at[k, 1], ("r2", k, 1), dn_y)

    def q_sum(k):
        arrive(q_r2.at[k, 0], ("r2", k, 0), dn_y)
        arrive(q_r2.at[k, 1], ("r2", k, 1), up_y)
        at = pl.ds(pl.multiple_of(y * 64, 64), 64)
        return q_part[k, at, :] + q_r2[k, 0].astype(F32) + q_r2[k, 1].astype(F32)

    def q_leave(k):
        q_s3[k - 1] = q_sum(k).astype(BF)
        send(q_s3.at[k - 1], q_r3.at[3 - k], ("r3", 4 - k), peer(0, k))

    def q_end():
        total = q_sum(0)
        for k in (1, 3, 2):
            arrive(q_r3.at[k - 1], ("r3", k), peer(0, k))
            total = total + q_r3[k - 1].astype(F32)
        qg_ref[...] = total.astype(BF)

    c_dot(0)
    q_dot(1)
    q_dot(2)
    c_mid(0)
    q_mid(1)
    c_dot(1)
    q_mid(2)
    q_dot(3)
    q_dot(0)
    c_mid(1)
    q_mid(3)
    q_leave(1)
    c_leave()
    q_mid(0)
    q_leave(2)
    q_leave(3)
    c_pass()
    q_end()
    c_end()
    wires.finish()


def local(queries, candidates, grades, query_weights):
    vmem = pl.BlockSpec(memory_space=pltpu.VMEM)
    weights = query_weights.reshape(4, 4, 2, 64).transpose(2, 1, 0, 3).reshape(16, LANES)
    shapes = [
        ((2048, 1024), BF), ((1024, 1024), BF), ((1024, 1024), BF), ((4, 128, 1024), jnp.int32),
        ((1024, 2048), jnp.int32), ((1024, 2048), F32), ((1024, 2048), BF), ((1024, 1024), BF),
        ((2, 64, 1024), BF), ((8, LANES), F32), ((16, 8, LANES), F32), ((16, 16, LANES), F32),
        ((16, 16, LANES), F32), ((2, 16, LANES), F32), ((16, 16, LANES), F32),
        ((4, 256, 1024), F32), ((4, 2, 32, 1024), BF), ((4, 2, 32, 1024), BF), ((4, 2, 64, 1024), BF),
        ((4, 2, 64, 1024), BF), ((3, 64, 1024), BF), ((3, 64, 1024), BF),
        ((2, 512, 1024), F32), ((2, 2, 64, 1024), BF), ((2, 2, 64, 1024), BF), ((2, 2, 128, 1024), BF),
        ((2, 2, 128, 1024), BF), ((128, 1024), BF), ((2, 64, 1024), BF), ((128, 1024), BF),
    ]
    losses, query_grad, cand_grad = pl.pallas_call(
        kernel,
        out_shape=(
            jax.ShapeDtypeStruct((16, LANES), F32),
            jax.ShapeDtypeStruct((64, 1024), BF),
            jax.ShapeDtypeStruct((128, 1024), BF),
        ),
        in_specs=[vmem, vmem, vmem, pl.BlockSpec(memory_space=pl.ANY)],
        out_specs=(vmem, vmem, vmem),
        scratch_shapes=[pltpu.VMEM(shape, dtype) for shape, dtype in shapes]
        + [
            pltpu.SemaphoreType.DMA((160,)),
            pltpu.SemaphoreType.DMA((160,)),
            pltpu.SemaphoreType.DMA((4, 2)),
        ],
        compiler_params=pltpu.CompilerParams(
            collective_id=0, has_side_effects=True, vmem_limit_bytes=66 * 1000 * 1000
        ),
        name="listmle",
    )(queries, candidates, weights, grades)
    losses = losses.reshape(2, 4, 4, 64).transpose(2, 1, 0, 3).reshape(2048)
    return losses, query_grad, cand_grad


def solution(mesh):
    split = Mesh(mesh.devices.reshape(2, 4, 4, 4, 2), AXES)
    return jax.shard_map(
        local,
        mesh=split,
        in_specs=(P(AXES_Q := ROWS + COL, None), P(COL + ROWS, None), P(ROWS, COL), P(ROWS)),
        out_specs=(P(ROWS), P(AXES_Q, None), P(COL + ROWS, None)),
        check_vma=False,
    )
```

time: 383 us -> 156 us (0.41)
  waiting for transfers between devices: 258 us -> 0 us
  Pallas kernels: 0 us -> 148 us
  other arithmetic: 35.9 us -> 0 us
  matrix products: 33.4 us -> 0 us
  blocking collectives: 30.4 us -> 0 us
  between operations: 14.2 us -> 0.64 us
    pallas_call x0 -> x1, Pallas kernels: none -> 148 us  [local(): pl.pallas_call(kernel, out_shape=(jax.ShapeDtypeStruct((16, LANES), F32),...]
    all_gather x2 -> x0, waiting for transfers between devices: 142 us -> none  [the longest x1 78.8 us: local(): cand_block = lax.all_gather(candidates, 'pb', axis=0, tiled=True)]
    ppermute x6 -> x0, waiting for transfers between devices: 101 us -> none  [partner(): lax.ppermute(x, axis, [(i, i ^ 1 << stride) for i in range(lax.axis_size(...]
    dot_general x3 -> x0, matrix products: 33.4 us -> none  [the longest x1 19.5 us: local(): jnp.dot(query_block, cand_block.T, preferred_element_type=jnp.float32)]
    all_gather x3 -> x0, blocking collectives: 30.4 us -> none  [all_in_one(): both, at, found = (lax.all_gather(jnp.concatenate(lines), axis), 0, {})]
    reduce_sum x1 -> x0, other arithmetic: 19.6 us -> none  [masses_from(): jnp.sum(jnp.where(members[bucket], expo, 0.0), axis=1)]
    reduce_scatter x1 -> x0, waiting for transfers between devices: 13.3 us -> none  [local(): lax.psum_scatter(lax.dot_general(slopes, query_block, (((0,), (0,)), ((),...]
    convert_element_type x3 -> x0, other arithmetic: 12.4 us -> none  [the longest x1 9.92 us: local(): (query_weights[:, None] * (spread_rows(scaled_factors) * expo - 1.0)).ast...]
  transfers between devices with their start and end apart: 9 -> 0, of which waited for: 8 -> 0; matrix products, arithmetic and copies ran while one was open for 4% -> 0% of each run, Pallas kernels for 0% -> 0%
where the time goes in v1:
time: 156 us; the launch traced here: 155 us
  Pallas kernels  148 us (95%)
  local copies, waits for them, and re-layouts  6.16 us (4%)
    pallas_call x1, Pallas kernels, local(): pl.pallas_call(kernel, out_shape=(jax.ShapeDtypeStruct((16, LANES), F32),...  148 us
    unnamed x2, local copies, waits for them, and re-layouts  3.24 us

profile of v1, /device:TPU:1, one launch (start us, length us, event | category | flops | bytes accessed | tf_op | source)
XLA Modules:
  0.0 155.0 jit_solution(9612206988284350902)
XLA Ops:
  0.6 0.8 reshape.18
  1.4 0.7 reshape.19.w_ref
  2.1 148.2 %listmle.1 = (f32[16,128]{1,0:T(8,128)}, bf16[64,1024]{1,0:T(8,128)(2,1)}, bf16[128,1024]{1,0:T(8,128)(2,1)}) custom-call(bf16[64,1024]{1,0:T(8,128)(2,1)} %q_ref.1, bf16[128,1024]{1,0:T(8,128)(2,1)} %c_ref.1, f32[16,128]{1,0:T(8,128)} %reshape.19.w_ref, s32[2048,1024]{1,0:T(8,128)} %g_hbm.1), custom_call_target="tpu_custom_call" | custom-call | tf_op jit(solution)/shard_map/listmle/pallas_call | solution.py:513
  150.3 0.8 reshape.20
  151.1 0.7 reshape.21
  151.8 1.6 %copy.13 = bf16[64,1024]{1,0:T(8,128)(2,1)} copy(bf16[64,1024]{1,0:T(8,128)(2,1)} %get-tuple-element.13) | data formatting | bytes 262144
  153.4 1.7 %copy.14 = bf16[128,1024]{1,0:T(8,128)(2,1)} copy(bf16[128,1024]{1,0:T(8,128)(2,1)} %get-tuple-element.14) | data formatting | bytes 524288
  (2 shorter events, 0.0 us)

commit v2 on v1

--- a/solution.py
+++ b/solution.py
@@ -102,13 +102,36 @@
     return stacked(maxima), stacked(factors + [losses])
 
 
+GATHER = lax.GatherDimensionNumbers(
+    offset_dims=(),
+    collapsed_slice_dims=(0,),
+    start_index_map=(0,),
+    operand_batching_dims=(1,),
+    start_indices_batching_dims=(1,),
+)
+
+
 def spread(table, grade):
-    return jnp.take_along_axis(table, grade, axis=0, mode="promise_in_bounds")
+    pieces = [
+        lax.gather(
+            table,
+            grade[at : at + 8][..., None],
+            GATHER,
+            slice_sizes=(1, 1),
+            mode=lax.GatherScatterMode.PROMISE_IN_BOUNDS,
+        )
+        for at in range(0, grade.shape[0], 8)
+    ]
+    return jnp.concatenate(pieces, axis=0)
+
+
+def folded(op, block):
+    return op(block.reshape(-1, 8, LANES), axis=0)
 
 
 def kernel(
     q_ref, c_ref, w_ref, g_hbm, loss_ref, qg_ref, cg_ref,
-    q_all, c_all, c_par, g_in, g_t, es, sl, sl_par, z_rel, tab, cnt, st, st_in, st_core, res,
+    q_all, c_all, c_par, w_t, g_in, g_t, es, sl, sl_par, z_rel, cnt, st_half, st, st_in, st_core, res,
     q_part, q_s1, q_r1, q_s2, q_r2, q_s3, q_r3,
     c_part, c_s1, c_r1, c_s2, c_r2, c_s3, c_rel, c_r3,
     send_sems, recv_sems, g_sems,
@@ -121,6 +144,7 @@
     up_x, dn_x = {"x": (x + 1) % 4}, {"x": (x + 3) % 4}
     mate = {"c": other}
     zl2 = (zl + 2) % 4
+    planes = (zl, zl + 1 - 2 * (zl % 2), zl2, 3 - zl)
     up_zh, dn_zh = (zh + zl // 2) % 2, (zh + 1 + zl // 2) % 2
     up_z, dn_z = {"zh": up_zh, "zl": zl2}, {"zh": dn_zh, "zl": zl2}
 
@@ -130,7 +154,7 @@
     others = [(dy, dz) for dy in range(4) for dz in range(4) if (dy, dz) != (0, 0)]
 
     def q_rows(core, k, dy, start=0, size=64):
-        at = core * 1024 + (zl + k) % 4 * 256 + (y + dy) % 4 * 64 + start
+        at = core * 1024 + planes[k] * 256 + (y + dy) % 4 * 64 + start
         return q_all.at[pl.ds(pl.multiple_of(at, 32), size), :]
 
     def c_rows(half, dx, start=0, size=128):
@@ -156,7 +180,7 @@
             copy.start()
 
     barrier = pltpu.get_barrier_semaphore()
-    greeted = [peer(dy, dz) for dy, dz in others] + [up_x, dn_x, mate, {"zh": 1 - zh, "zl": zl2}]
+    greeted = [{"zl": planes[k]} for k in (1, 2, 3)] + [up_y, dn_y, up_x, dn_x, mate, {"zh": 1 - zh, "zl": zl2}]
     for device in greeted:
         pl.semaphore_signal(barrier, inc=1, device_id=device, device_id_type=pl.DeviceIdType.MESH)
     pl.semaphore_wait(barrier, len(greeted))
@@ -167,9 +191,14 @@
     send(c_ref, c_rows(zh, 0), ("cx", 1), dn_x)
     send(c_ref.at[pl.ds(0, 64), :], z_rel.at[0], ("zr", 0), up_z)
     send(c_ref.at[pl.ds(64, 64), :], z_rel.at[1], ("zr", 1), dn_z)
-    for m in (1, 3, 2):
-        send(q_ref, q_rows(c, 0, 0), ("qz", 4 - m), peer(0, m))
+    for k in (1, 2, 3):
+        send(q_ref, q_rows(c, 0, 0), ("qz", k), {"zl": planes[k]})
     send(q_ref, q_rows(c, 0, 0), ("qd", 0, 0), mate)
+    for t in range(16):
+        core, at = t // 8, t % 2 * 8 + t // 2 % 4
+        pair = [w_ref[pl.ds(at, 1), :], w_ref[pl.ds(at + 4, 1), :]]
+        pair[1 - core] = pltpu.roll(pair[1 - core], 64, 1)
+        w_t[pl.ds(t, 1), :] = jnp.where(lax.broadcasted_iota(jnp.int32, (1, LANES), 1) < 64, *pair)
     q_rows(c, 0, 0)[...] = q_ref[...]
     c_rows(zh, 0)[...] = c_ref[...]
 
@@ -190,7 +219,7 @@
         to_mate(k, 2)
 
     def q_over(k):
-        arrive(q_rows(c, k, 0), ("qz", k), peer(0, k))
+        arrive(q_rows(c, k, 0), ("qz", k), {"zl": planes[k]})
         send(q_rows(c, k, 0), q_rows(c, k, 0), ("qy", k, 0), up_y)
         send(q_rows(c, k, 0), q_rows(c, k, 0), ("qy", k, 1), dn_y)
         to_mate(k, 0)
@@ -243,82 +272,91 @@
             for copy in grade_copies(tile + 4):
                 copy.start()
 
-        def tally(i, held):
-            held = list(held)
-            for j in range(8):
-                at = pl.multiple_of(i * 64 + 8 * j, 8)
-                grade = g_t[pl.ds(at, 8), pl.ds(128 * tile, 128)]
-                for k in range(4):
-                    held[k] = held[k] + jnp.where(grade == k, 1.0, 0.0)
-            return tuple(held)
-
-        held = lax.fori_loop(0, 16, tally, (jnp.zeros((8, LANES), F32),) * 4)
-        held = [jnp.sum(v, axis=0, keepdims=True) for v in held]
-        held.append(1024.0 - (held[0] + held[1] + held[2] + held[3]))
-        cnt[tile] = stacked(held)
-
-    steps = [
-        lambda: q_near(0), c_near, c_relay, lambda: q_over(1), lambda: q_over(3), lambda: q_far(0), c_far,
-        lambda: q_over(2), lambda: q_near(1), lambda: q_near(3), c_over, lambda: q_near(2), p_near,
-        lambda: q_far(1), lambda: q_far(3), lambda: q_far(2), p_far,
-    ]
-    for n, step in enumerate(steps):
-        if n < 16:
-            turn(n)
-        step()
-    send(c_all, c_par, ("cp",), mate)
-    for k in range(4):
-        for dy in range(4):
-            arrive(q_rows(other, k, dy), ("qd", k, dy), mate)
-
-    tab[...] = jnp.zeros_like(tab)
-
-    def tile_stats(tile):
+        for h in range(2):
+
+            def tally(i, held):
+                at = pl.ds(pl.multiple_of(h * 512 + i * 64, 64), 64)
+                grade = g_t[at, pl.ds(128 * tile, 128)]
+                return tuple(v + folded(jnp.sum, jnp.where(grade == k, 1.0, 0.0)) for k, v in enumerate(held))
+
+            held = lax.fori_loop(0, 8, tally, (jnp.zeros((8, LANES), F32),) * 4)
+            held = [jnp.sum(v, axis=0, keepdims=True) for v in held]
+            held.append(512.0 - (held[0] + held[1] + held[2] + held[3]))
+            cnt[h, tile] = stacked(held)
+
+    def tile_stats(half, tile):
         lanes = pl.ds(pl.multiple_of(tile * LANES, LANES), LANES)
 
         def highest(i, held):
-            held = list(held)
-            for j in range(8):
-                at = pl.ds(pl.multiple_of(i * 64 + 8 * j, 8), 8)
-                score, grade = es[at, lanes], g_t[at, lanes]
-                for k in range(GRADES):
-                    held[k] = jnp.maximum(held[k], jnp.where(grade == k, score, 32.0 * LOWEST))
-                held[GRADES] = held[GRADES] + score
-            return tuple(held)
+            at = pl.ds(pl.multiple_of(half * 512 + i * 64, 64), 64)
+            score, grade = es[at, lanes], g_t[at, lanes]
+            new = [
+                jnp.maximum(held[k], folded(jnp.max, jnp.where(grade == k, score, 32.0 * LOWEST)))
+                for k in range(GRADES)
+            ]
+            return (*new, held[GRADES] + folded(jnp.sum, score))
 
         low = jnp.full((8, LANES), 32.0 * LOWEST, F32)
-        held = lax.fori_loop(0, 16, highest, (low,) * GRADES + (jnp.zeros((8, LANES), F32),))
+        held = lax.fori_loop(0, 8, highest, (low,) * GRADES + (jnp.zeros((8, LANES), F32),))
         maxima = [jnp.max(v, axis=0, keepdims=True) for v in held[:GRADES]]
         total = jnp.sum(held[GRADES], axis=0, keepdims=True) * SCALE
         table = stacked(maxima)
 
         def masses_of(i, held):
-            held = list(held)
-            for j in range(8):
-                at = pl.ds(pl.multiple_of(i * 64 + 8 * j, 8), 8)
-                score, grade = es[at, lanes], g_t[at, lanes]
-                value = jnp.exp2((score - spread(table, grade)) * EXP2_SCALE)
-                es[at, lanes] = value
-                for k in range(GRADES):
-                    held[k] = held[k] + jnp.where(grade == k, value, 0.0)
-            return tuple(held)
-
-        held = lax.fori_loop(0, 16, masses_of, (jnp.zeros((8, LANES), F32),) * GRADES)
+            at = pl.ds(pl.multiple_of(half * 512 + i * 64, 64), 64)
+            score, grade = es[at, lanes], g_t[at, lanes]
+            value = jnp.exp2((score - spread(table, grade)) * EXP2_SCALE)
+            es[at, lanes] = value
+            return tuple(
+                held[k] + folded(jnp.sum, jnp.where(grade == k, value, 0.0)) for k in range(GRADES)
+            )
+
+        held = lax.fori_loop(0, 8, masses_of, (jnp.zeros((8, LANES), F32),) * GRADES)
         masses = [jnp.sum(v, axis=0, keepdims=True) for v in held]
-        counts = [cnt[tile, pl.ds(k, 1), :] for k in range(GRADES)]
-        st[tile, pl.ds(0, 8), :] = stacked([m * SCALE for m in maxima] + counts[:3])
-        st[tile, pl.ds(8, 8), :] = stacked(masses + counts[3:] + [total])
-
-    def score_tile(n, _):
-        rows = pl.ds(pl.multiple_of(n * 256, 256), 256)
-        es[:, rows] = lax.dot_general(
-            c_all[...], q_all[rows, :], (((1,), (1,)), ((), ())), preferred_element_type=F32
+        counts = [cnt[half, tile, pl.ds(k, 1), :] for k in range(GRADES)]
+        st_half[half, tile, pl.ds(0, 8), :] = stacked([m * SCALE for m in maxima] + counts[:3])
+        st_half[half, tile, pl.ds(8, 8), :] = stacked(masses + counts[3:] + [total])
+
+    def unit(h, k):
+        half = (zh + h) % 2
+        cands = pl.ds(pl.multiple_of(half * 512, 512), 512)
+
+        def one(core, _):
+            n = core * 4 + planes[k]
+            rows = pl.ds(pl.multiple_of(n * 256, 256), 256)
+            es[cands, rows] = lax.dot_general(
+                c_all[cands, :], q_all[rows, :], (((1,), (1,)), ((), ())), preferred_element_type=F32
+            )
+            tile_stats(half, 2 * n)
+            tile_stats(half, 2 * n + 1)
+            return 0
+
+        lax.fori_loop(0, 2, one, 0)
+
+    def turns(first, last):
+        for tile in range(first, last):
+            turn(tile)
+
+    def q_mate(k):
+        for dy in range(4):
+            arrive(q_rows(other, k, dy), ("qd", k, dy), mate)
+
+    steps = [
+        (turns, 0, 8), (q_near, 0), (turns, 8, 12), (c_near,), (c_relay,), (turns, 12, 16), (q_over, 1), (q_far, 0),
+        (c_far,), (q_mate, 0), (unit, 0, 0), (q_over, 2), (q_near, 1), (c_over,), (q_over, 3), (q_far, 1), (q_near, 2),
+        (p_near,), (q_near, 3), (q_mate, 1), (unit, 0, 1), (q_far, 2), (p_far,),
+        (send, c_all, c_par, ("cp",), mate), (q_mate, 2), (unit, 0, 2), (unit, 1, 0), (q_far, 3), (unit, 1, 1),
+        (q_mate, 3), (unit, 0, 3), (unit, 1, 2), (unit, 1, 3),
+    ]
+    for step, *given in steps:
+        step(*given)
+
+    for t in range(16):
+        first, second = combine(
+            [(st_half[h, t, pl.ds(0, 8), :], st_half[h, t, pl.ds(8, 8), :]) for h in range(2)]
         )
-        tile_stats(2 * n)
-        tile_stats(2 * n + 1)
-        return 0
-
-    lax.fori_loop(0, 8, score_tile, 0)
+        st[t, pl.ds(0, 8), :] = first
+        st[t, pl.ds(8, 8), :] = second
 
     mine = y * 4 + zl
     for dy, dz in others:
@@ -343,40 +381,46 @@
     for dy, dz in others:
         source = (y + 4 - dy) % 4 * 4 + (zl + 4 - dz) % 4
         arrive(res.at[source], ("sr", dy, dz), peer(4 - dy, 4 - dz))
-    loss_ref[...] = res[:, 13, :]
-
-    def slope_tile(tile):
+    found = [res[t, pl.ds(13, 1), :] for t in range(16)]
+    low_lanes = lax.broadcasted_iota(jnp.int32, (1, LANES), 1) < 64
+    for v in range(4):
+        for p in range(4):
+            pair = [found[core * 8 + p * 2 + v // 2] for core in range(2)]
+            pair[1 - v % 2] = pltpu.roll(pair[1 - v % 2], 64, 1)
+            loss_ref[pl.ds(v * 4 + p, 1), :] = jnp.where(low_lanes, pair[0], pair[1])
+
+    def slope_tile(half, tile):
         lanes = pl.ds(pl.multiple_of(tile * LANES, LANES), LANES)
-        weight = w_ref[pl.ds(tile, 1), :] * SCALE
-        table = res[tile, pl.ds(8, 8), :] * jnp.exp(st[tile, pl.ds(0, 8), :] - res[tile, pl.ds(0, 8), :])
+        weight = w_t[pl.ds(tile, 1), :] * SCALE
+        table = res[tile, pl.ds(8, 8), :] * jnp.exp(st_half[half, tile, pl.ds(0, 8), :] - res[tile, pl.ds(0, 8), :])
         row = lax.broadcasted_iota(jnp.int32, (8, LANES), 0)
         table = jnp.where(row < GRADES, table, 0.0) * weight
 
         def at_rows(i, _):
-            for j in range(4):
-                at = pl.multiple_of(i * 64 + 16 * j, 16)
-                halves = []
-                for h in range(2):
-                    rows = pl.ds(pl.multiple_of(at + 8 * h, 8), 8)
-                    halves.append(spread(table, g_t[rows, lanes]) * es[rows, lanes] - weight)
-                sl[pl.ds(at, 16), lanes] = jnp.concatenate(halves, axis=0).astype(BF)
+            at = pl.ds(pl.multiple_of(half * 512 + i * 64, 64), 64)
+            sl[at, lanes] = (spread(table, g_t[at, lanes]) * es[at, lanes] - weight).astype(BF)
             return 0
 
-        lax.fori_loop(0, 16, at_rows, 0)
+        lax.fori_loop(0, 8, at_rows, 0)
 
     def lanes_of(core, plane):
         return pl.ds(pl.multiple_of(core * 1024 + plane * 256, 256), 256)
 
-    for k in (1, 2, 3, 0):
-        plane = (zl + k) % 4
-        slope_tile(other * 8 + plane * 2)
-        slope_tile(other * 8 + plane * 2 + 1)
-        lanes = lanes_of(other, plane)
-        send(sl.at[:, lanes], sl_par.at[:, lanes_of(0, plane)], ("sl", k), mate)
-    for k in (1, 2, 3, 0):
-        plane = (zl + k) % 4
-        slope_tile(c * 8 + plane * 2)
-        slope_tile(c * 8 + plane * 2 + 1)
+    def slopes(j):
+        half = (zh + 1 - j) % 2
+        cands = pl.ds(pl.multiple_of(half * 512, 512), 512)
+
+        def one(t, core):
+            slope_tile(half, core * 8 + t)
+            return core
+
+        lax.fori_loop(0, 8, one, other)
+        send(sl.at[cands, pl.ds(pl.multiple_of(other * 1024, 1024), 1024)], sl_par.at[cands, :], ("sl", j), mate)
+        lax.fori_loop(0, 8, one, c)
+
+    def slopes_mate(j):
+        cands = pl.ds(pl.multiple_of((zh + 1 - j) % 2 * 512, 512), 512)
+        arrive(sl_par.at[cands, :], ("sl", j), mate)
 
     def c_dot(j):
         half = (zh + 1 - j) % 2
@@ -431,8 +475,7 @@
     dims = (((0,), (0,)), ((), ()))
 
     def q_dot(k):
-        plane = (zl + k) % 4
-        arrive(sl_par.at[:, lanes_of(0, plane)], ("sl", k), mate)
+        plane = planes[k]
         q_part[k] = lax.dot_general(
             sl[:, lanes_of(c, plane)], c_all[...], dims, preferred_element_type=F32
         ) + lax.dot_general(sl_par[:, lanes_of(0, plane)], c_par[...], dims, preferred_element_type=F32)
@@ -466,44 +509,32 @@
 
     def q_leave(k):
         q_s3[k - 1] = q_sum(k).astype(BF)
-        send(q_s3.at[k - 1], q_r3.at[3 - k], ("r3", 4 - k), peer(0, k))
+        send(q_s3.at[k - 1], q_r3.at[k - 1], ("r3", k), {"zl": planes[k]})
 
     def q_end():
         total = q_sum(0)
-        for k in (1, 3, 2):
-            arrive(q_r3.at[k - 1], ("r3", k), peer(0, k))
+        for k in (1, 2, 3):
+            arrive(q_r3.at[k - 1], ("r3", k), {"zl": planes[k]})
             total = total + q_r3[k - 1].astype(F32)
         qg_ref[...] = total.astype(BF)
 
-    c_dot(0)
-    q_dot(1)
-    q_dot(2)
-    c_mid(0)
-    q_mid(1)
-    c_dot(1)
-    q_mid(2)
-    q_dot(3)
-    q_dot(0)
-    c_mid(1)
-    q_mid(3)
-    q_leave(1)
-    c_leave()
-    q_mid(0)
-    q_leave(2)
-    q_leave(3)
-    c_pass()
-    q_end()
-    c_end()
+    steps = [
+        (slopes, 0), (c_dot, 0), (slopes, 1), (slopes_mate, 0), (slopes_mate, 1), (q_dot, 1), (c_mid, 0), (q_dot, 2),
+        (q_mid, 1), (q_dot, 3), (c_dot, 1), (q_mid, 2), (q_leave, 1), (c_leave,), (q_dot, 0), (q_mid, 3), (c_mid, 1),
+        (q_leave, 2), (q_mid, 0), (q_leave, 3), (c_pass,), (q_end,), (c_end,),
+    ]
+    for step, *given in steps:
+        step(*given)
     wires.finish()
 
 
 def local(queries, candidates, grades, query_weights):
     vmem = pl.BlockSpec(memory_space=pltpu.VMEM)
-    weights = query_weights.reshape(4, 4, 2, 64).transpose(2, 1, 0, 3).reshape(16, LANES)
+    weights = query_weights.reshape(16, LANES)
     shapes = [
-        ((2048, 1024), BF), ((1024, 1024), BF), ((1024, 1024), BF), ((4, 128, 1024), jnp.int32),
+        ((2048, 1024), BF), ((1024, 1024), BF), ((1024, 1024), BF), ((16, LANES), F32), ((4, 128, 1024), jnp.int32),
         ((1024, 2048), jnp.int32), ((1024, 2048), F32), ((1024, 2048), BF), ((1024, 1024), BF),
-        ((2, 64, 1024), BF), ((8, LANES), F32), ((16, 8, LANES), F32), ((16, 16, LANES), F32),
+        ((2, 64, 1024), BF), ((2, 16, 8, LANES), F32), ((2, 16, 16, LANES), F32), ((16, 16, LANES), F32),
         ((16, 16, LANES), F32), ((2, 16, LANES), F32), ((16, 16, LANES), F32),
         ((4, 256, 1024), F32), ((4, 2, 32, 1024), BF), ((4, 2, 32, 1024), BF), ((4, 2, 64, 1024), BF),
         ((4, 2, 64, 1024), BF), ((3, 64, 1024), BF), ((3, 64, 1024), BF),
@@ -530,8 +561,7 @@
         ),
         name="listmle",
     )(queries, candidates, weights, grades)
-    losses = losses.reshape(2, 4, 4, 64).transpose(2, 1, 0, 3).reshape(2048)
-    return losses, query_grad, cand_grad
+    return losses.reshape(2048), query_grad, cand_grad
 
 
 def solution(mesh):

time: 156 us -> 131 us (0.84)
  Pallas kernels: 148 us -> 125 us
  local copies, waits for them, and re-layouts: 6.16 us -> 4.53 us
    pallas_call x1, Pallas kernels: 148 us -> 125 us  [local(): pl.pallas_call(kernel, out_shape=(jax.ShapeDtypeStruct((16, LANES), F32),...]
    reshape x5 -> x0, local copies, waits for them, and re-layouts: 2.92 us -> none  [the longest x3 1.47 us: local(): losses = losses.reshape(2, 4, 4, 64).transpose(2, 1, 0, 3).reshape(2048)]
    unnamed x2 -> x3, local copies, waits for them, and re-layouts: 3.24 us -> 4.53 us
where the time goes in v2:
time: 131 us; the launch traced here: 130 us
  Pallas kernels  125 us (95%)
  local copies, waits for them, and re-layouts  4.53 us (3%)
    pallas_call x1, Pallas kernels, local(): pl.pallas_call(kernel, out_shape=(jax.ShapeDtypeStruct((16, LANES), F32),...  125 us
    unnamed x3, local copies, waits for them, and re-layouts  4.53 us

profile of v2, /device:TPU:1, one launch (start us, length us, event | category | flops | bytes accessed | tf_op | source)
XLA Modules:
  0.0 130.4 jit_solution(11061938270031933024)
XLA Ops:
  0.6 125.2 %listmle.1 = (f32[16,128]{1,0:T(8,128)}, bf16[64,1024]{1,0:T(8,128)(2,1)}, bf16[128,1024]{1,0:T(8,128)(2,1)}) custom-call(bf16[64,1024]{1,0:T(8,128)(2,1)} %q_ref.1, bf16[128,1024]{1,0:T(8,128)(2,1)} %c_ref.1, f32[16,128]{1,0:T(8,128)} %bitcast.2, s32[2048,1024]{1,0:T(8,128)} %g_hbm.1), custom_call_target="tpu_custom_call" | custom-call | tf_op jit(solution)/shard_map/listmle/pallas_call | solution.py:544
  125.9 1.3 copy.10
  127.2 1.6 %copy.11 = bf16[64,1024]{1,0:T(8,128)(2,1)} copy(bf16[64,1024]{1,0:T(8,128)(2,1)} %get-tuple-element.13) | data formatting | bytes 262144
  128.7 1.7 %copy.12 = bf16[128,1024]{1,0:T(8,128)(2,1)} copy(bf16[128,1024]{1,0:T(8,128)(2,1)} %get-tuple-element.14) | data formatting | bytes 524288

commit v3 on v2

v3 whole, which is shorter than its diff:
```python
import jax
import jax.numpy as jnp
from jax import lax
from jax.experimental import pallas as pl
from jax.experimental.pallas import tpu as pltpu
from jax.sharding import Mesh
from jax.sharding import PartitionSpec as P

GRADES = 5
LOWEST = -1e30
AXES = ("zh", "x", "y", "zl", "c")
ROWS = ("zh", "x")
COL = ("y", "zl", "c")
SCALE = 1.0 / 32.0
EXP2_SCALE = 1.4426950408889634 / 32.0
BF = jnp.bfloat16
F32 = jnp.float32
LANES = 128


class Wires:
    def __init__(self, send_sems, recv_sems):
        self.send_sems, self.recv_sems = send_sems, recv_sems
        self.names, self.sent = {}, []

    def slot(self, name):
        return self.names.setdefault(name, len(self.names))

    def send(self, src, dst, name, where):
        copy = pltpu.make_async_remote_copy(
            src_ref=src,
            dst_ref=dst,
            send_sem=self.send_sems.at[len(self.sent)],
            recv_sem=self.recv_sems.at[self.slot(name)],
            device_id=where,
            device_id_type=pl.DeviceIdType.MESH,
        )
        copy.start()
        self.sent.append(copy)

    def arrive(self, dst, name, where):
        pltpu.make_async_remote_copy(
            src_ref=dst,
            dst_ref=dst,
            send_sem=self.send_sems.at[0],
            recv_sem=self.recv_sems.at[self.slot(name)],
            device_id=where,
            device_id_type=pl.DeviceIdType.MESH,
        ).wait_recv()

    def finish(self):
        for copy in self.sent:
            copy.wait_send()


def combine(parts):
    row = lax.broadcasted_iota(jnp.int32, (8, LANES), 0)
    stat = row < GRADES
    top = parts[0][0]
    for first, _ in parts[1:]:
        top = jnp.maximum(top, first)
    plain = jnp.zeros((8, LANES), F32)
    mass = jnp.zeros((8, LANES), F32)
    for first, second in parts:
        plain = plain + first
        mass = mass + second * jnp.where(stat, jnp.exp(first - top), 1.0)
    return jnp.where(stat, top, plain), mass


def stacked(rows):
    row = lax.broadcasted_iota(jnp.int32, (8, LANES), 0)
    out = jnp.zeros((8, LANES), F32)
    for k, value in enumerate(rows):
        out = jnp.where(row == k, value, out)
    return out


def outcome(first, second, columns):
    maxima = [first[k : k + 1] for k in range(GRADES)]
    masses = [second[k : k + 1] for k in range(GRADES)]
    counts = [first[5:6], first[6:7], first[7:8], second[5:6], second[6:7]]
    totals = second[7:8]
    levels, running, seen = [], maxima[0], jnp.zeros_like(totals)
    for k in range(GRADES):
        running = jnp.maximum(running, maxima[k])
        seen = seen + counts[k]
        summed = masses[0] * jnp.exp(maxima[0] - running)
        for h in range(1, k + 1):
            summed = summed + masses[h] * jnp.exp(maxima[h] - running)
        present = seen > 0.0
        levels.append(jnp.where(present, running + jnp.log(jnp.where(present, summed, 1.0)), running))
    weighted = counts[0] * levels[0]
    for k in range(1, GRADES):
        weighted = weighted + counts[k] * levels[k]
    losses = (weighted - totals) / columns
    factors = []
    for h in range(GRADES):
        summed = counts[h] * jnp.exp(maxima[h] - levels[h])
        for k in range(h + 1, GRADES):
            summed = summed + counts[k] * jnp.exp(maxima[h] - levels[k])
        factors.append(summed)
    return stacked(maxima), stacked(factors + [losses])


GATHER = lax.GatherDimensionNumbers(
    offset_dims=(),
    collapsed_slice_dims=(0,),
    start_index_map=(0,),
    operand_batching_dims=(1,),
    start_indices_batching_dims=(1,),
)


def spread(table, grade):
    pieces = [
        lax.gather(
            table,
            grade[at : at + 8][..., None],
            GATHER,
            slice_sizes=(1, 1),
            mode=lax.GatherScatterMode.PROMISE_IN_BOUNDS,
        )
        for at in range(0, grade.shape[0], 8)
    ]
    return jnp.concatenate(pieces, axis=0)


def folded(op, block):
    return op(block.reshape(-1, 8, LANES), axis=0)


def kernel(
    q_hbm, c_hbm, w_hbm, g_hbm, loss_ref, qg_ref, cg_ref,
    q_all, c_all, c_par, w_ref, w_t, g_in, g_t, es, sl, sl_par, z_rel, cnt, st_half, st, st_in, st_core, res,
    q_part, q_s1, q_r1, q_s2, q_r2, q_s3, q_r3,
    c_part, c_s1, c_r1, c_s2, c_r2, c_s3, c_rel, c_r3,
    send_sems, recv_sems, g_sems, in_sems,
):
    zh, x, y, zl, c = (lax.axis_index(a) for a in AXES)
    other = 1 - c
    wires = Wires(send_sems, recv_sems)
    send, arrive = wires.send, wires.arrive
    up_y, dn_y = {"y": (y + 1) % 4}, {"y": (y + 3) % 4}
    up_x, dn_x = {"x": (x + 1) % 4}, {"x": (x + 3) % 4}
    mate = {"c": other}
    zl2 = (zl + 2) % 4
    planes = (zl, zl + 1 - 2 * (zl % 2), zl2, 3 - zl)
    up_zh, dn_zh = (zh + zl // 2) % 2, (zh + 1 + zl // 2) % 2
    up_z, dn_z = {"zh": up_zh, "zl": zl2}, {"zh": dn_zh, "zl": zl2}

    def q_rows(core, k, dy, start=0, size=64):
        at = core * 1024 + planes[k] * 256 + (y + dy) % 4 * 64 + start
        return q_all.at[pl.ds(pl.multiple_of(at, 32), size), :]

    def c_rows(half, dx, start=0, size=128):
        at = half * 512 + (x + dx) % 4 * 128 + start
        return c_all.at[pl.ds(pl.multiple_of(at, 32), size), :]

    own = [
        pltpu.make_async_copy(q_hbm, q_rows(c, 0, 0), in_sems.at[0]),
        pltpu.make_async_copy(c_hbm, c_rows(zh, 0), in_sems.at[1]),
        pltpu.make_async_copy(w_hbm, w_ref, in_sems.at[2]),
    ]
    for copy in own:
        copy.start()

    def grade_copies(tile):
        core, plane, pair = tile // 8, tile // 2 % 4, tile % 2
        copies = []
        for i in range(2):
            at = (((pair * 2 + i) * 4 + plane) * 2 + core) * 64
            copies.append(
                pltpu.make_async_copy(
                    g_hbm.at[pl.ds(at, 64), :],
                    g_in.at[tile % 4, pl.ds(64 * i, 64), :],
                    g_sems.at[tile % 4, i],
                )
            )
        return copies

    for tile in range(4):
        for copy in grade_copies(tile):
            copy.start()

    barrier = pltpu.get_barrier_semaphore()
    greeted = [{"zl": planes[k]} for k in (1, 2, 3)] + [up_y, dn_y, up_x, dn_x, mate, {"zh": 1 - zh, "zl": zl2}]
    for device in greeted:
        pl.semaphore_signal(barrier, inc=1, device_id=device, device_id_type=pl.DeviceIdType.MESH)
    pl.semaphore_wait(barrier, len(greeted))

    for copy in own:
        copy.wait()
    q_own, c_own = q_rows(c, 0, 0), c_rows(zh, 0)
    for i in range(2):
        for h, where in ((0, up_z), (1, dn_z)):
            send(c_rows(zh, 0, 64 * h + 32 * i, 32), z_rel.at[h, pl.ds(32 * i, 32), :], ("zr", h, i), where)
    send(q_own, q_own, ("qy", 0, 0), up_y)
    send(q_own, q_own, ("qy", 0, 1), dn_y)
    send(c_own, c_own, ("cx", 0), up_x)
    send(c_own, c_own, ("cx", 1), dn_x)
    send(q_own, q_own, ("qz", 2), {"zl": planes[2]})
    send(q_own, q_own, ("qd", 0, 0), mate)
    for t in range(16):
        core, at = t // 8, t % 2 * 8 + t // 2 % 4
        pair = [w_ref[pl.ds(at, 1), :], w_ref[pl.ds(at + 4, 1), :]]
        pair[1 - core] = pltpu.roll(pair[1 - core], 64, 1)
        w_t[pl.ds(t, 1), :] = jnp.where(lax.broadcasted_iota(jnp.int32, (1, LANES), 1) < 64, *pair)

    def to_mate(k, dy):
        send(q_rows(c, k, dy), q_rows(c, k, dy), ("qd", k, dy), mate)

    def q_near(k):
        arrive(q_rows(c, k, 3), ("qy", k, 0), dn_y)
        send(q_rows(c, k, 3, 0, 32), q_rows(c, k, 3, 0, 32), ("qf", k, 0), up_y)
        to_mate(k, 3)
        arrive(q_rows(c, k, 1), ("qy", k, 1), up_y)
        send(q_rows(c, k, 1, 32, 32), q_rows(c, k, 1, 32, 32), ("qf", k, 1), dn_y)
        to_mate(k, 1)

    def q_far(k):
        arrive(q_rows(c, k, 2, 0, 32), ("qf", k, 0), dn_y)
        arrive(q_rows(c, k, 2, 32, 32), ("qf", k, 1), up_y)
        to_mate(k, 2)

    def q_over(k):
        arrive(q_rows(c, k, 0), ("qz", k), {"zl": planes[k if k < 3 else 1]})
        send(q_rows(c, k, 0), q_rows(c, k, 0), ("qy", k, 0), up_y)
        send(q_rows(c, k, 0), q_rows(c, k, 0), ("qy", k, 1), dn_y)
        if k == 2:
            send(q_rows(c, k, 0), q_rows(c, k, 0), ("qz", 3), {"zl": planes[1]})
        to_mate(k, 0)

    def c_near():
        arrive(c_rows(zh, 3), ("cx", 0), dn_x)
        send(c_rows(zh, 3, 0, 64), c_rows(zh, 3, 0, 64), ("cf", 0), up_x)
        arrive(c_rows(zh, 1), ("cx", 1), up_x)
        send(c_rows(zh, 1, 64, 64), c_rows(zh, 1, 64, 64), ("cf", 1), dn_x)

    def c_far():
        arrive(c_rows(zh, 2, 0, 64), ("cf", 0), dn_x)
        arrive(c_rows(zh, 2, 64, 64), ("cf", 1), up_x)

    def c_relay(i):
        for h, frm, where, there in ((0, dn_z, up_z, up_zh), (1, up_z, dn_z, dn_zh)):
            part = z_rel.at[h, pl.ds(32 * i, 32), :]
            arrive(part, ("zr", h, i), frm)
            send(part, c_rows(1 - there, 0, 64 * h + 32 * i, 32), ("cz", h, i), where)

    def q_leap():
        send(q_own, q_own, ("qz", 1), {"zl": planes[1]})

    def c_over(i):
        for h, frm in ((0, dn_z), (1, up_z)):
            part = c_rows(1 - zh, 0, 64 * h + 32 * i, 32)
            arrive(part, ("cz", h, i), frm)
            send(part, part, ("px", h, i, 0), up_x)
            send(part, part, ("px", h, i, 1), dn_x)

    def p_near(i):
        for h in range(2):
            below, above = c_rows(1 - zh, 3, 64 * h + 32 * i, 32), c_rows(1 - zh, 1, 64 * h + 32 * i, 32)
            arrive(below, ("px", h, i, 0), dn_x)
            if h == 0:
                send(below, below, ("pf", 0, i), up_x)
            arrive(above, ("px", h, i, 1), up_x)
            if h == 1:
                send(above, above, ("pf", 1, i), dn_x)

    def p_far():
        for i in range(2):
            for h, frm in ((0, dn_x), (1, up_x)):
                arrive(c_rows(1 - zh, 2, 64 * h + 32 * i, 32), ("pf", h, i), frm)

    def turn(tile):
        for copy in grade_copies(tile):
            copy.wait()
        for b in range(8):
            block = g_in[tile % 4, :, pl.ds(128 * b, 128)]
            g_t[pl.ds(128 * b, 128), pl.ds(128 * tile, 128)] = jnp.transpose(block)
        if tile + 4 < 16:
            for copy in grade_copies(tile + 4):
                copy.start()

        for h in range(2):

            def tally(i, held):
                at = pl.ds(pl.multiple_of(h * 512 + i * 64, 64), 64)
                grade = g_t[at, pl.ds(128 * tile, 128)]
                return tuple(v + folded(jnp.sum, jnp.where(grade == k, 1.0, 0.0)) for k, v in enumerate(held))

            held = lax.fori_loop(0, 8, tally, (jnp.zeros((8, LANES), F32),) * 4)
            held = [jnp.sum(v, axis=0, keepdims=True) for v in held]
            held.append(512.0 - (held[0] + held[1] + held[2] + held[3]))
            cnt[h, tile] = stacked(held)

    def pair_stats(half, first):
        lanes = [pl.ds(pl.multiple_of((first + i) * LANES, LANES), LANES) for i in range(2)]
        zero = jnp.zeros((8, LANES), F32)
        low = jnp.full((8, LANES), 32.0 * LOWEST, F32)

        def highest(n, held):
            at = pl.ds(pl.multiple_of(half * 512 + n * 64, 64), 64)
            new = []
            for i in range(2):
                score, grade = es[at, lanes[i]], g_t[at, lanes[i]]
                for k in range(GRADES):
                    found = folded(jnp.max, jnp.where(grade == k, score, 32.0 * LOWEST))
                    new.append(jnp.maximum(held[6 * i + k], found))
                new.append(held[6 * i + GRADES] + folded(jnp.sum, score))
            return tuple(new)

        held = lax.fori_loop(0, 8, highest, ((low,) * GRADES + (zero,)) * 2)
        maxima = [[jnp.max(v, axis=0, keepdims=True) for v in held[6 * i : 6 * i + GRADES]] for i in range(2)]
        total = [jnp.sum(held[6 * i + GRADES], axis=0, keepdims=True) * SCALE for i in range(2)]
        tables = [stacked(m) for m in maxima]

        def masses_of(n, held):
            at = pl.ds(pl.multiple_of(half * 512 + n * 64, 64), 64)
            new, values = [], []
            for i in range(2):
                score, grade = es[at, lanes[i]], g_t[at, lanes[i]]
                value = jnp.exp2((score - spread(tables[i], grade)) * EXP2_SCALE)
                values.append(value)
                for k in range(GRADES):
                    new.append(held[5 * i + k] + folded(jnp.sum, jnp.where(grade == k, value, 0.0)))
            for i in range(2):
                es[at, lanes[i]] = values[i]
            return tuple(new)

        held = lax.fori_loop(0, 8, masses_of, (zero,) * (2 * GRADES))
        for i in range(2):
            masses = [jnp.sum(v, axis=0, keepdims=True) for v in held[5 * i : 5 * i + GRADES]]
            counts = [cnt[half, first + i, pl.ds(k, 1), :] for k in range(GRADES)]
            st_half[half, first + i, pl.ds(0, 8), :] = stacked([m * SCALE for m in maxima[i]] + counts[:3])
            st_half[half, first + i, pl.ds(8, 8), :] = stacked(masses + counts[3:] + [total[i]])

    def unit(h, k):
        half = (zh + h) % 2
        cands = pl.ds(pl.multiple_of(half * 512, 512), 512)

        def one(core, _):
            n = core * 4 + planes[k]
            rows = pl.ds(pl.multiple_of(n * 256, 256), 256)
            es[cands, rows] = lax.dot_general(
                c_all[cands, :], q_all[rows, :], (((1,), (1,)), ((), ())), preferred_element_type=F32
            )
            pair_stats(half, 2 * n)
            return 0

        lax.fori_loop(0, 2, one, 0)

    columns = (y, y + 1 - 2 * (y % 2), (y + 2) % 4, 3 - y)
    slots = [(d, k) for k in range(4) for d in range(4)]

    def tile_of(d, k):
        return columns[d] // 2 * 8 + planes[k] * 2 + columns[d] % 2

    def chip(d, k):
        return {"y": columns[d], "zl": planes[k]}

    def st_out(k):
        for d in range(4):
            t, n = tile_of(d, k), k * 4 + d
            first, second = combine(
                [(st_half[h, t, pl.ds(0, 8), :], st_half[h, t, pl.ds(8, 8), :]) for h in range(2)]
            )
            st[n, pl.ds(0, 8), :] = first
            st[n, pl.ds(8, 8), :] = second
        for d in range(4):
            if (d, k) != (0, 0):
                n = k * 4 + d
                send(st.at[n], st_in.at[n], ("st", d, k), chip(d, k))

    def turns(first, last):
        for tile in range(first, last):
            turn(tile)

    def q_mate(k):
        for dy in range(4):
            arrive(q_rows(other, k, dy), ("qd", k, dy), mate)

    steps = [
        (turns, 0, 6), (q_near, 0), (c_relay, 0), (turns, 6, 8), (c_near,), (c_relay, 1), (q_leap,), (turns, 8, 11),
        (q_over, 2), (q_far, 0), (c_far,), (turns, 11, 13), (c_over, 0), (turns, 13, 16), (q_mate, 0), (c_over, 1), (q_near, 2),
        (p_near, 0), (q_over, 1), (unit, 0, 0), (p_near, 1), (q_over, 3), (q_far, 2), (q_mate, 2), (unit, 0, 2), (q_near, 1),
        (p_far,), (send, c_all, c_par, ("cp",), mate), (q_near, 3), (unit, 1, 0), (st_out, 0), (q_far, 1), (unit, 1, 2),
        (st_out, 2), (q_mate, 1), (q_far, 3), (unit, 0, 1), (unit, 1, 1), (st_out, 1), (q_mate, 3), (unit, 0, 3), (unit, 1, 3),
        (st_out, 3),
    ]
    for step, *given in steps:
        step(*given)

    mine = tile_of(0, 0)
    parts = [(st[0, pl.ds(0, 8), :], st[0, pl.ds(8, 8), :])]
    for d, k in slots[1:]:
        n = k * 4 + d
        arrive(st_in.at[n], ("st", d, k), chip(d, k))
        parts.append((st_in[n, pl.ds(0, 8), :], st_in[n, pl.ds(8, 8), :]))
    first, second = combine(parts)
    st_core[0, pl.ds(0, 8), :] = first
    st_core[0, pl.ds(8, 8), :] = second
    send(st_core.at[0], st_core.at[1], ("sd",), mate)
    arrive(st_core.at[1], ("sd",), mate)
    first, second = combine([(first, second), (st_core[1, pl.ds(0, 8), :], st_core[1, pl.ds(8, 8), :])])
    first, second = outcome(first, second, 32768.0)
    res[mine, pl.ds(0, 8), :] = first
    res[mine, pl.ds(8, 8), :] = second
    for d, k in reversed(slots[1:]):
        send(res.at[mine], res.at[mine], ("sr", d, k), chip(d, k))
    arrive(c_par, ("cp",), mate)
    for d, k in slots[1:]:
        arrive(res.at[tile_of(d, k)], ("sr", d, k), chip(d, k))
    found = [res[t, pl.ds(13, 1), :] for t in range(16)]
    low_lanes = lax.broadcasted_iota(jnp.int32, (1, LANES), 1) < 64
    for v in range(4):
        for p in range(4):
            pair = [found[core * 8 + p * 2 + v // 2] for core in range(2)]
            pair[1 - v % 2] = pltpu.roll(pair[1 - v % 2], 64, 1)
            loss_ref[pl.ds(v * 4 + p, 1), :] = jnp.where(low_lanes, pair[0], pair[1])

    row = lax.broadcasted_iota(jnp.int32, (8, LANES), 0)
    for t in range(16):
        weight = w_t[pl.ds(t, 1), :] * SCALE
        for h in range(2):
            table = res[t, pl.ds(8, 8), :] * jnp.exp(st_half[h, t, pl.ds(0, 8), :] - res[t, pl.ds(0, 8), :])
            table = jnp.where(row < GRADES, table, 0.0) * weight
            st_half[h, t, pl.ds(8, 8), :] = jnp.where(row == 7, weight, table)

    def slope_block(j, d):
        half = (zh + 1 - j) % 2
        at = pl.ds(pl.multiple_of(half * 512 + (x + d) % 4 * 128, 128), 128)

        def one(t, _):
            lanes = pl.ds(pl.multiple_of(t * LANES, LANES), LANES)
            table = st_half[half, t, pl.ds(8, 8), :]
            sl[at, lanes] = (spread(table, g_t[at, lanes]) * es[at, lanes] - table[7:8]).astype(BF)
            return 0

        lax.fori_loop(0, 16, one, 0)

    def slopes_out(j):
        cands = pl.ds(pl.multiple_of((zh + 1 - j) % 2 * 512, 512), 512)
        send(sl.at[cands, pl.ds(pl.multiple_of(other * 1024, 1024), 1024)], sl_par.at[cands, :], ("sl", j), mate)

    def lanes_of(core, plane):
        return pl.ds(pl.multiple_of(core * 1024 + plane * 256, 256), 256)

    def slopes_mate(j):
        cands = pl.ds(pl.multiple_of((zh + 1 - j) % 2 * 512, 512), 512)
        arrive(sl_par.at[cands, :], ("sl", j), mate)

    def c_block(d, start=0, size=128):
        return pl.ds(pl.multiple_of((x + d) % 4 * 128 + start, 32), size)

    def c_dot(j, d):
        at = pl.multiple_of((zh + 1 - j) % 2 * 512 + (x + d) % 4 * 128, 128)
        c_part[j, c_block(d), :] = jnp.dot(sl[pl.ds(at, 128), :], q_all[...], preferred_element_type=F32)

    def c_far_part(j):
        c_dot(j, 2)
        for side in range(2):
            c_s1[j, side] = c_part[j, c_block(2, 64 * side, 64), :].astype(BF)
        for i in range(2):
            for side, where in ((0, up_x), (1, dn_x)):
                at = pl.ds(32 * i, 32)
                send(c_s1.at[j, side, at, :], c_r1.at[j, side, at, :], ("s1", j, side, i), where)

    def c_rest(j):
        for d, side in ((1, 0), (3, 1)):
            c_dot(j, d)
            at = pl.ds(64 - 64 * side, 64)
            c_s2[j, side, at, :] = c_part[j, c_block(d, 64 - 64 * side, 64), :].astype(BF)
        for i in range(2):
            for side, where in ((0, up_x), (1, dn_x)):
                at = pl.ds(64 - 64 * side + 32 * i, 32)
                send(c_s2.at[j, side, at, :], c_r2.at[j, side, at, :], ("s2", j, side, i), where)

    def c_mid(j, i):
        for d, side, frm, where in ((1, 0, dn_x, up_x), (3, 1, up_x, dn_x)):
            half = pl.ds(32 * i, 32)
            arrive(c_r1.at[j, side, half, :], ("s1", j, side, i), frm)
            at = pl.ds(64 * side + 32 * i, 32)
            own_part = c_part[j, c_block(d, 64 * side + 32 * i, 32), :]
            c_s2[j, side, at, :] = (own_part + c_r1[j, side, half, :].astype(F32)).astype(BF)
            send(c_s2.at[j, side, at, :], c_r2.at[j, side, at, :], ("s4", j, side, i), where)

    def c_take(j, i):
        for side, frm in ((0, dn_x), (1, up_x)):
            arrive(c_r2.at[j, side, pl.ds(64 - 64 * side + 32 * i, 32), :], ("s2", j, side, i), frm)
            arrive(c_r2.at[j, side, pl.ds(64 * side + 32 * i, 32), :], ("s4", j, side, i), frm)

    def c_leave(i):
        c_take(0, i)
        for h, where in ((0, up_z), (1, dn_z)):
            at = pl.ds(64 * h + 32 * i, 32)
            total = c_part[0, c_block(0, 64 * h + 32 * i, 32), :] + c_r2[0, 0, at, :].astype(F32) + c_r2[0, 1, at, :].astype(F32)
            c_s3[at, :] = total.astype(BF)
            send(c_s3.at[at, :], c_rel.at[h, pl.ds(32 * i, 32), :], ("t1", h, i), where)

    def c_pass(i):
        for h, frm, where in ((0, dn_z, up_z), (1, up_z, dn_z)):
            part = c_rel.at[h, pl.ds(32 * i, 32), :]
            arrive(part, ("t1", h, i), frm)
            send(part, c_r3.at[pl.ds(64 * h + 32 * i, 32), :], ("t2", h, i), where)

    def c_end():
        for i in range(2):
            c_take(1, i)
        total = c_part[1, c_block(0), :] + c_r2[1, 0].astype(F32) + c_r2[1, 1].astype(F32)
        for i in range(2):
            for h, frm in ((0, dn_z), (1, up_z)):
                arrive(c_r3.at[pl.ds(64 * h + 32 * i, 32), :], ("t2", h, i), frm)
        cg_ref[...] = (total + c_r3[...].astype(F32)).astype(BF)

    dims = (((0,), (0,)), ((), ()))

    def q_block(d, start, size):
        return pl.ds(pl.multiple_of((y + d) % 4 * 64 + start, 32), size)

    def q_dot(k):
        plane = planes[k]
        q_part[k] = lax.dot_general(
            sl[:, lanes_of(c, plane)], c_all[...], dims, preferred_element_type=F32
        ) + lax.dot_general(sl_par[:, lanes_of(0, plane)], c_par[...], dims, preferred_element_type=F32)

        q_s1[k, 0] = q_part[k, q_block(2, 0, 32), :].astype(BF)
        q_s1[k, 1] = q_part[k, q_block(2, 32, 32), :].astype(BF)
        send(q_s1.at[k, 0], q_r1.at[k, 0], ("r1", k, 0), up_y)
        send(q_s1.at[k, 1], q_r1.at[k, 1], ("r1", k, 1), dn_y)
        for d, side, where in ((1, 0, up_y), (3, 1, dn_y)):
            at = pl.ds(32 - 32 * side, 32)
            q_s2[k, side, at, :] = q_part[k, q_block(d, 32 - 32 * side, 32), :].astype(BF)
            send(q_s2.at[k, side, at, :], q_r2.at[k, side, at, :], ("r2", k, side), where)

    def q_mid(k):
        for d, side, frm, where in ((1, 0, dn_y, up_y), (3, 1, up_y, dn_y)):
            arrive(q_r1.at[k, side], ("r1", k, side), frm)
            at = pl.ds(32 * side, 32)
            q_s2[k, side, at, :] = (q_part[k, q_block(d, 32 * side, 32), :] + q_r1[k, side].astype(F32)).astype(BF)
            send(q_s2.at[k, side, at, :], q_r2.at[k, side, at, :], ("r4", k, side), where)

    def q_sum(k):
        for side, frm in ((0, dn_y), (1, up_y)):
            arrive(q_r2.at[k, side, pl.ds(32 - 32 * side, 32), :], ("r2", k, side), frm)
            arrive(q_r2.at[k, side, pl.ds(32 * side, 32), :], ("r4", k, side), frm)
        at = pl.ds(pl.multiple_of(y * 64, 64), 64)
        return q_part[k, at, :] + q_r2[k, 0].astype(F32) + q_r2[k, 1].astype(F32)

    def q_leave(k):
        total = q_sum(k)
        if k == 2:
            arrive(q_r3.at[2], ("r3", 3), {"zl": planes[1]})
            total = total + q_r3[2].astype(F32)
        q_s3[k - 1] = total.astype(BF)
        send(q_s3.at[k - 1], q_r3.at[k - 1], ("r3", k), {"zl": planes[k if k < 3 else 1]})

    def q_end():
        total = q_sum(0)
        for k in (1, 2):
            arrive(q_r3.at[k - 1], ("r3", k), {"zl": planes[k]})
            total = total + q_r3[k - 1].astype(F32)
        qg_ref[...] = total.astype(BF)

    steps = [
        (slope_block, 0, 2), (c_far_part, 0), (slope_block, 0, 1), (slope_block, 0, 3), (c_rest, 0), (slope_block, 0, 0),
        (slopes_out, 0), (c_mid, 0, 0), (slope_block, 1, 0), (slope_block, 1, 1), (slope_block, 1, 2), (slope_block, 1, 3),
        (slopes_out, 1), (c_mid, 0, 1), (c_dot, 0, 0), (slopes_mate, 0), (slopes_mate, 1), (q_dot, 3), (c_leave, 0), (q_dot, 2),
        (q_mid, 3), (c_leave, 1), (q_dot, 1), (c_pass, 0), (q_mid, 2), (q_leave, 3), (c_pass, 1), (q_mid, 1), (c_far_part, 1),
        (c_rest, 1), (q_leave, 2), (q_dot, 0), (q_leave, 1), (c_mid, 1, 0), (c_mid, 1, 1), (c_dot, 1, 0), (q_mid, 0), (q_end,),
        (c_end,),
    ]
    for step, *given in steps:
        step(*given)
    wires.finish()


def local(queries, candidates, grades, query_weights):
    vmem = pl.BlockSpec(memory_space=pltpu.VMEM)
    weights = query_weights.reshape(16, LANES)
    shapes = [
        ((2048, 1024), BF), ((1024, 1024), BF), ((1024, 1024), BF), ((16, LANES), F32), ((16, LANES), F32), ((4, 128, 1024), jnp.int32),
        ((1024, 2048), jnp.int32), ((1024, 2048), F32), ((1024, 2048), BF), ((1024, 1024), BF),
        ((2, 64, 1024), BF), ((2, 16, 8, LANES), F32), ((2, 16, 16, LANES), F32), ((16, 16, LANES), F32),
        ((16, 16, LANES), F32), ((2, 16, LANES), F32), ((16, 16, LANES), F32),
        ((4, 256, 1024), F32), ((4, 2, 32, 1024), BF), ((4, 2, 32, 1024), BF), ((4, 2, 64, 1024), BF),
        ((4, 2, 64, 1024), BF), ((3, 64, 1024), BF), ((3, 64, 1024), BF),
        ((2, 512, 1024), F32), ((2, 2, 64, 1024), BF), ((2, 2, 64, 1024), BF), ((2, 2, 128, 1024), BF),
        ((2, 2, 128, 1024), BF), ((128, 1024), BF), ((2, 64, 1024), BF), ((128, 1024), BF),
    ]
    losses, query_grad, cand_grad = pl.pallas_call(
        kernel,
        out_shape=(
            jax.ShapeDtypeStruct((16, LANES), F32),
            jax.ShapeDtypeStruct((64, 1024), BF),
            jax.ShapeDtypeStruct((128, 1024), BF),
        ),
        in_specs=[pl.BlockSpec(memory_space=pl.ANY)] * 4,
        out_specs=(vmem, vmem, vmem),
        scratch_shapes=[pltpu.VMEM(shape, dtype) for shape, dtype in shapes]
        + [
            pltpu.SemaphoreType.DMA((192,)),
            pltpu.SemaphoreType.DMA((192,)),
            pltpu.SemaphoreType.DMA((4, 2)),
            pltpu.SemaphoreType.DMA((3,)),
        ],
        compiler_params=pltpu.CompilerParams(
            collective_id=0, has_side_effects=True, vmem_limit_bytes=66 * 1000 * 1000
        ),
        name="listmle",
    )(queries, candidates, weights, grades)
    return losses.reshape(2048), query_grad, cand_grad


def solution(mesh):
    split = Mesh(mesh.devices.reshape(2, 4, 4, 4, 2), AXES)
    return jax.shard_map(
        local,
        mesh=split,
        in_specs=(P(AXES_Q := ROWS + COL, None), P(COL + ROWS, None), P(ROWS, COL), P(ROWS)),
        out_specs=(P(ROWS), P(AXES_Q, None), P(COL + ROWS, None)),
        check_vma=False,
    )
```

time: 131 us -> 113 us (0.86)
  Pallas kernels: 125 us -> 108 us
    pallas_call x1, Pallas kernels: 125 us -> 108 us  [local(): pl.pallas_call(kernel, out_shape=(jax.ShapeDtypeStruct((16, LANES), F32),...]
where the time goes in v3:
time: 113 us
  Pallas kernels  108 us (96%)
  local copies, waits for them, and re-layouts  4.53 us (4%)
    pallas_call x1, Pallas kernels, local(): pl.pallas_call(kernel, out_shape=(jax.ShapeDtypeStruct((16, LANES), F32),...  108 us
    unnamed x3, local copies, waits for them, and re-layouts  4.53 us

profile of v3, /device:TPU:1, one launch (start us, length us, event | category | flops | bytes accessed | tf_op | source)
XLA Modules:
  0.0 113.3 jit_solution(85710776190580545)
XLA Ops:
  0.6 108.1 %listmle.1 = (f32[16,128]{1,0:T(8,128)}, bf16[64,1024]{1,0:T(8,128)(2,1)}, bf16[128,1024]{1,0:T(8,128)(2,1)}) custom-call(bf16[64,1024]{1,0:T(8,128)(2,1)} %q_hbm.1, bf16[128,1024]{1,0:T(8,128)(2,1)} %c_hbm.1, f32[16,128]{1,0:T(8,128)} %bitcast.2, s32[2048,1024]{1,0:T(8,128)} %g_hbm.1), custom_call_target="tpu_custom_call" | custom-call | tf_op jit(solution)/shard_map/listmle/pallas_call | solution.py:590
  108.7 1.3 %copy.10 = f32[2048]{0:T(1024)} copy(f32[2048]{0:T(1024)} %bitcast.3) | data formatting | bytes 16384
  110.0 1.6 %copy.11 = bf16[64,1024]{1,0:T(8,128)(2,1)} copy(bf16[64,1024]{1,0:T(8,128)(2,1)} %get-tuple-element.13) | data formatting | bytes 262144
  111.6 1.7 %copy.12 = bf16[128,1024]{1,0:T(8,128)(2,1)} copy(bf16[128,1024]{1,0:T(8,128)(2,1)} %get-tuple-element.14) | data formatting | bytes 524288

commit v4 on v3

--- a/solution.py
+++ b/solution.py
@@ -130,7 +130,7 @@
 
 
 def kernel(
-    q_hbm, c_hbm, w_hbm, g_hbm, loss_ref, qg_ref, cg_ref,
+    q_hbm, c_hbm, w_hbm, g_hbm, loss_ref, out_ref,
     q_all, c_all, c_par, w_ref, w_t, g_in, g_t, es, sl, sl_par, z_rel, cnt, st_half, st, st_in, st_core, res,
     q_part, q_s1, q_r1, q_s2, q_r2, q_s3, q_r3,
     c_part, c_s1, c_r1, c_s2, c_r2, c_s3, c_rel, c_r3,
@@ -309,7 +309,7 @@
                 new.append(held[6 * i + GRADES] + folded(jnp.sum, score))
             return tuple(new)
 
-        held = lax.fori_loop(0, 8, highest, ((low,) * GRADES + (zero,)) * 2)
+        held = lax.fori_loop(0, 8, highest, ((low,) * GRADES + (zero,)) * 2, unroll=2)
         maxima = [[jnp.max(v, axis=0, keepdims=True) for v in held[6 * i : 6 * i + GRADES]] for i in range(2)]
         total = [jnp.sum(held[6 * i + GRADES], axis=0, keepdims=True) * SCALE for i in range(2)]
         tables = [stacked(m) for m in maxima]
@@ -327,7 +327,7 @@
                 es[at, lanes[i]] = values[i]
             return tuple(new)
 
-        held = lax.fori_loop(0, 8, masses_of, (zero,) * (2 * GRADES))
+        held = lax.fori_loop(0, 8, masses_of, (zero,) * (2 * GRADES), unroll=2)
         for i in range(2):
             masses = [jnp.sum(v, axis=0, keepdims=True) for v in held[5 * i : 5 * i + GRADES]]
             counts = [cnt[half, first + i, pl.ds(k, 1), :] for k in range(GRADES)]
@@ -381,10 +381,10 @@
 
     steps = [
         (turns, 0, 6), (q_near, 0), (c_relay, 0), (turns, 6, 8), (c_near,), (c_relay, 1), (q_leap,), (turns, 8, 11),
-        (q_over, 2), (q_far, 0), (c_far,), (turns, 11, 13), (c_over, 0), (turns, 13, 16), (q_mate, 0), (c_over, 1), (q_near, 2),
-        (p_near, 0), (q_over, 1), (unit, 0, 0), (p_near, 1), (q_over, 3), (q_far, 2), (q_mate, 2), (unit, 0, 2), (q_near, 1),
-        (p_far,), (send, c_all, c_par, ("cp",), mate), (q_near, 3), (unit, 1, 0), (st_out, 0), (q_far, 1), (unit, 1, 2),
-        (st_out, 2), (q_mate, 1), (q_far, 3), (unit, 0, 1), (unit, 1, 1), (st_out, 1), (q_mate, 3), (unit, 0, 3), (unit, 1, 3),
+        (q_over, 2), (q_far, 0), (c_far,), (turns, 11, 13), (c_over, 0), (turns, 13, 16), (q_mate, 0), (c_over, 1),
+        (unit, 0, 0), (q_near, 2), (p_near, 0), (q_over, 1), (p_near, 1), (q_over, 3), (q_far, 2), (q_mate, 2), (unit, 0, 2),
+        (q_near, 1), (p_far,), (send, c_all, c_par, ("cp",), mate), (unit, 1, 0), (q_near, 3), (st_out, 0), (unit, 1, 2), (q_far, 1),
+        (st_out, 2), (q_far, 3), (q_mate, 1), (unit, 0, 1), (unit, 1, 1), (st_out, 1), (q_mate, 3), (unit, 0, 3), (unit, 1, 3),
         (st_out, 3),
     ]
     for step, *given in steps:
@@ -410,13 +410,15 @@
     arrive(c_par, ("cp",), mate)
     for d, k in slots[1:]:
         arrive(res.at[tile_of(d, k)], ("sr", d, k), chip(d, k))
-    found = [res[t, pl.ds(13, 1), :] for t in range(16)]
-    low_lanes = lax.broadcasted_iota(jnp.int32, (1, LANES), 1) < 64
-    for v in range(4):
-        for p in range(4):
-            pair = [found[core * 8 + p * 2 + v // 2] for core in range(2)]
-            pair[1 - v % 2] = pltpu.roll(pair[1 - v % 2], 64, 1)
-            loss_ref[pl.ds(v * 4 + p, 1), :] = jnp.where(low_lanes, pair[0], pair[1])
+    def losses_out():
+        found = [res[t, pl.ds(13, 1), :] for t in range(16)]
+        low_lanes = lax.broadcasted_iota(jnp.int32, (1, LANES), 1) < 64
+        for v in range(4):
+            for p in range(4):
+                pair = [found[core * 8 + p * 2 + v // 2] for core in range(2)]
+                pair[1 - v % 2] = pltpu.roll(pair[1 - v % 2], 64, 1)
+                loss_ref[pl.ds(v * 4 + p, 1), :] = jnp.where(low_lanes, pair[0], pair[1])
+        loss_ref[pl.ds(16, 8), :] = jnp.zeros((8, LANES), F32)
 
     row = lax.broadcasted_iota(jnp.int32, (8, LANES), 0)
     for t in range(16):
@@ -436,7 +438,7 @@
             sl[at, lanes] = (spread(table, g_t[at, lanes]) * es[at, lanes] - table[7:8]).astype(BF)
             return 0
 
-        lax.fori_loop(0, 16, one, 0)
+        lax.fori_loop(0, 16, one, 0, unroll=2)
 
     def slopes_out(j):
         cands = pl.ds(pl.multiple_of((zh + 1 - j) % 2 * 512, 512), 512)
@@ -510,7 +512,7 @@
         for i in range(2):
             for h, frm in ((0, dn_z), (1, up_z)):
                 arrive(c_r3.at[pl.ds(64 * h + 32 * i, 32), :], ("t2", h, i), frm)
-        cg_ref[...] = (total + c_r3[...].astype(F32)).astype(BF)
+        out_ref[pl.ds(64, 128), :] = total + c_r3[...].astype(F32)
 
     dims = (((0,), (0,)), ((), ()))
 
@@ -559,15 +561,15 @@
         for k in (1, 2):
             arrive(q_r3.at[k - 1], ("r3", k), {"zl": planes[k]})
             total = total + q_r3[k - 1].astype(F32)
-        qg_ref[...] = total.astype(BF)
+        out_ref[pl.ds(0, 64), :] = total
 
     steps = [
         (slope_block, 0, 2), (c_far_part, 0), (slope_block, 0, 1), (slope_block, 0, 3), (c_rest, 0), (slope_block, 0, 0),
         (slopes_out, 0), (c_mid, 0, 0), (slope_block, 1, 0), (slope_block, 1, 1), (slope_block, 1, 2), (slope_block, 1, 3),
         (slopes_out, 1), (c_mid, 0, 1), (c_dot, 0, 0), (slopes_mate, 0), (slopes_mate, 1), (q_dot, 3), (c_leave, 0), (q_dot, 2),
-        (q_mid, 3), (c_leave, 1), (q_dot, 1), (c_pass, 0), (q_mid, 2), (q_leave, 3), (c_pass, 1), (q_mid, 1), (c_far_part, 1),
-        (c_rest, 1), (q_leave, 2), (q_dot, 0), (q_leave, 1), (c_mid, 1, 0), (c_mid, 1, 1), (c_dot, 1, 0), (q_mid, 0), (q_end,),
-        (c_end,),
+        (q_mid, 3), (c_leave, 1), (q_dot, 1), (c_pass, 0), (q_mid, 2), (q_leave, 3), (q_dot, 0), (c_pass, 1), (q_mid, 1),
+        (c_far_part, 1), (c_rest, 1), (q_leave, 1), (q_leave, 2), (c_mid, 1, 0), (c_mid, 1, 1), (c_dot, 1, 0), (q_mid, 0),
+        (losses_out,), (q_end,), (c_end,),
     ]
     for step, *given in steps:
         step(*given)
@@ -587,15 +589,11 @@
         ((2, 512, 1024), F32), ((2, 2, 64, 1024), BF), ((2, 2, 64, 1024), BF), ((2, 2, 128, 1024), BF),
         ((2, 2, 128, 1024), BF), ((128, 1024), BF), ((2, 64, 1024), BF), ((128, 1024), BF),
     ]
-    losses, query_grad, cand_grad = pl.pallas_call(
+    losses, out = pl.pallas_call(
         kernel,
-        out_shape=(
-            jax.ShapeDtypeStruct((16, LANES), F32),
-            jax.ShapeDtypeStruct((64, 1024), BF),
-            jax.ShapeDtypeStruct((128, 1024), BF),
-        ),
+        out_shape=(jax.ShapeDtypeStruct((24, LANES), F32), jax.ShapeDtypeStruct((192, 1024), F32)),
         in_specs=[pl.BlockSpec(memory_space=pl.ANY)] * 4,
-        out_specs=(vmem, vmem, vmem),
+        out_specs=(vmem, vmem),
         scratch_shapes=[pltpu.VMEM(shape, dtype) for shape, dtype in shapes]
         + [
             pltpu.SemaphoreType.DMA((192,)),
@@ -608,7 +606,7 @@
         ),
         name="listmle",
     )(queries, candidates, weights, grades)
-    return losses.reshape(2048), query_grad, cand_grad
+    return losses[:16].reshape(2048), out[:64].astype(BF), out[64:].astype(BF)
 
 
 def solution(mesh):

time: 113 us -> 113 us (level)
  local copies, waits for them, and re-layouts: 4.53 us -> 2.68 us
  other arithmetic: 0 us -> 1.18 us
    unnamed x3 -> x0, local copies, waits for them, and re-layouts: 4.53 us -> none
    slice x0 -> x2, local copies, waits for them, and re-layouts: none -> 1.38 us  [local(): return (losses[:16].reshape(2048), out[:64].astype(BF), out[64:].astype(BF))]
    reshape x0 -> x1, local copies, waits for them, and re-layouts: none -> 1.3 us  [local(): return (losses[:16].reshape(2048), out[:64].astype(BF), out[64:].astype(BF))]
    another operation x0 -> x1, other arithmetic: none -> 1.18 us
where the time goes in v4:
time: 113 us; the launch traced here: 112 us
  Pallas kernels  108 us (96%)
  local copies, waits for them, and re-layouts  2.68 us (2%)
  other arithmetic  1.18 us (1%)
    pallas_call x1, Pallas kernels, local(): pl.pallas_call(kernel, out_shape=(jax.ShapeDtypeStruct((24, LANES), F32),...  108 us

profile of v4, /device:TPU:1, one launch (start us, length us, event | category | flops | bytes accessed | tf_op | source)
XLA Modules:
  0.0 112.4 jit_solution(7808893986223131269)
XLA Ops:
  0.6 107.9 %listmle.1 = (f32[24,128]{1,0:T(8,128)}, f32[192,1024]{1,0:T(8,128)}) custom-call(bf16[64,1024]{1,0:T(8,128)(2,1)} %q_hbm.1, bf16[128,1024]{1,0:T(8,128)(2,1)} %c_hbm.1, f32[16,128]{1,0:T(8,128)} %bitcast.3, s32[2048,1024]{1,0:T(8,128)} %g_hbm.1), custom_call_target="tpu_custom_call" | custom-call | tf_op jit(solution)/shard_map/listmle/pallas_call | solution.py:592
  108.6 1.3 %slice_bitcast_fusion = f32[2048]{0:T(1024)} fusion(f32[24,128]{1,0:T(8,128)} %get-tuple-element.5), kind=kLoop, calls=%fused_computation | loop fusion | bytes 16384 | tf_op jit(solution)/shard_map/reshape | solution.py:609
  109.9 1.2 %convert.4 = bf16[192,1024]{1,0:T(8,128)(2,1)S(1)} convert(f32[192,1024]{1,0:T(8,128)} %get-tuple-element.6) | non-fusion elementwise | flops 196608 | bytes 1179648 | tf_op jit(solution)/shard_map/convert.1
  111.0 0.7 slice.14
  111.7 0.7 slice.15
